TPU v7x, 32 devices: a whole 2x2x4 slice. The times are simulated.
32 devices in a mesh: dp: 8 (over z, y), tensor: 4 (over x, core).
Axes of the slice: x: 2, y: 2, z: 4, core: 2. Of those that a mesh axis runs over, the one named last changes fastest.
Arguments:
- layer_in: bfloat16 [24576, 768], P(('dp', 'tensor')), may hold values from -6 to 6
- prompt_len: int32 [8], P('dp'), may hold values from 512 to 1024, as said below
- cont_len: int32 [8, 8], P('dp'), may hold values from 128 to 256, as said below
- w_qkv: bfloat16 [3, 768, 768], P(None, None, 'tensor'), may hold values from -0.21875 to 0.21875
- b_qv: bfloat16 [2, 768], P(None, 'tensor'), may hold values from -3 to 3
- w_proj: bfloat16 [768, 768], P('tensor'), may hold values from -1.75 to 1.75
- b_proj: bfloat16 [768], replicated, may hold values from -2 to 2
- ln1_gain: bfloat16 [768], replicated, may hold values from 0.25 to 1.75
- ln1_bias: bfloat16 [768], replicated, may hold values from -2 to 2
- ln2_gain: bfloat16 [768], replicated, may hold values from 0.25 to 1.75
- ln2_bias: bfloat16 [768], replicated, may hold values from -2 to 2
- w_in: bfloat16 [768, 3072], P(None, 'tensor'), may hold values from -0.21875 to 0.21875
- b_in: bfloat16 [3072], P('tensor'), may hold values from -2 to 2
- w_out: bfloat16 [3072, 768], P('tensor'), may hold values from -0.109375 to 0.109375
- b_out: bfloat16 [768], replicated, may hold values from -2 to 2
- out_grad: bfloat16 [24576, 768], P(('dp', 'tensor')), may hold values from -6 to 6
Outputs:
- layer_out: bfloat16 [24576, 768], P(('dp', 'tensor'))
- in_grad: float32 [24576, 768], P(('dp', 'tensor'))
- grad_w_qkv: float32 [3, 768, 768], P(None, None, 'tensor')
- grad_b_qv: float32 [2, 768], P(None, 'tensor')
- grad_w_proj: float32 [768, 768], P('tensor')
- grad_b_proj: float32 [768], replicated
- grad_ln1_gain: float32 [768], replicated
- grad_ln1_bias: float32 [768], replicated
- grad_ln2_gain: float32 [768], replicated
- grad_ln2_bias: float32 [768], replicated
- grad_w_in: float32 [768, 3072], P(None, 'tensor')
- grad_b_in: float32 [3072], P('tensor')
- grad_w_out: float32 [3072, 768], P('tensor')
- grad_b_out: float32 [768], replicated
Inputs may be any that keep to these rules, and one draw needn't show every extreme that they name: `prompt_len`: in every draw some group's prompt has all 1024 rows valid. `cont_len`: in every group some continuation has all 256 rows valid.
All inputs are finite; a program needn't handle non-finite values.
Results may differ from a plain program's by a relative error of at most 0.018.
Values may be sent and summed in bfloat16 or wider, within the bound.
A program may use at most 192 MiB of HBM per device.

v0:
```python
import functools

import jax
import jax.numpy as jnp
from jax import lax
from jax.experimental import pallas as pl
from jax.experimental.pallas import tpu as pltpu
from jax.sharding import PartitionSpec as P

HEAD = 64
PROMPT = 1024
CONT = 8
CLEN = 256
PIECES = 4
MESH = pl.DeviceIdType.MESH
ANY = pl.BlockSpec(memory_space=pl.ANY)

EPS = 1e-06
MASKED = -1000000000.0
BF = jnp.bfloat16
F32 = jnp.float32


def nt(a, b):
    return lax.dot_general(a, b, (((1,), (1,)), ((), ())), preferred_element_type=F32)


def nn(a, b):
    return lax.dot_general(a, b, (((1,), (0,)), ((), ())), preferred_element_type=F32)


def tn(a, b):
    return lax.dot_general(a, b, (((0,), (0,)), ((), ())), preferred_element_type=F32)


NEAR = 8


class Peers:
    def __init__(self):
        self.t = lax.axis_index("tensor")
        self.d = lax.axis_index("dp")
        self.odd = lax.rem(self.t, 2)
        self.p = lax.rem(self.d, 2)
        self.z = lax.div(lax.rem(self.d, NEAR), 2)
        self.base = self.d - lax.rem(self.d, NEAR)
        self.core = {"tensor": self.t + 1 - 2 * self.odd}
        self.x = {"tensor": lax.rem(self.t + 2, 4)}
        self.y = {"dp": self.d + 1 - 2 * self.p}

    def along(self, k, count):
        return {"dp": self.base + lax.rem(self.z + k, count) * 2 + self.p}


def enter(devices):
    barrier = pltpu.get_barrier_semaphore()
    for device in devices:
        pl.semaphore_signal(barrier, inc=1, device_id=device, device_id_type=MESH)
    pl.semaphore_wait(barrier, len(devices))


def remote(src, dst, send, recv, device):
    return pltpu.make_async_remote_copy(
        src_ref=src, dst_ref=dst, send_sem=send, recv_sem=recv, device_id=device, device_id_type=MESH
    )


def beyond(value):
    size = lax.axis_size("dp")
    step = NEAR
    while step < size:
        value = value + lax.ppermute(value, "dp", [(i, i ^ step) for i in range(size)])
        step *= 2
    return value


def own_lanes(rows, h):
    lane = lax.broadcasted_iota(jnp.int32, (rows, 128), 1)
    return ((lane < 64) if h == 0 else (lane >= 64)), lane - (64 if h == 0 else 0)


def key_aug(k, h, length, base):
    rows = k.shape[0]
    own, extra = own_lanes(rows, h)
    row = lax.broadcasted_iota(jnp.int32, (rows, 128), 0) + base
    bias = jnp.where(jnp.logical_and(extra == 0, row >= length), MASKED, 0.0)
    return jnp.where(own, k.astype(F32), bias).astype(BF)


def query_aug(q, h):
    own, extra = own_lanes(q.shape[0], h)
    return jnp.where(own, q.astype(F32) * 0.125, jnp.where(extra == 0, 1.0, 0.0)).astype(BF)


def value_aug(v, h):
    own, extra = own_lanes(v.shape[0], h)
    ones = jnp.where(jnp.logical_and(extra >= 0, extra < 3), 1.0, 0.0)
    return jnp.where(own, v.astype(F32), ones).astype(BF)


def transposed(v):
    return v.astype(F32).T


def wide_keys(k, length, base):
    rows = k.shape[0]
    lane = lax.broadcasted_iota(jnp.int32, (rows, 128), 1)
    row = lax.broadcasted_iota(jnp.int32, (rows, 128), 0) + base
    bias = jnp.where(jnp.logical_and(lane == 0, row >= length), MASKED, 0.0).astype(BF)
    return jnp.concatenate([k, bias], axis=1)


def wide_values(v):
    lane = lax.broadcasted_iota(jnp.int32, v.shape, 1)
    return jnp.concatenate([v, jnp.where(lane < 3, 1.0, 0.0).astype(BF)], axis=1)


def wide_queries(q):
    lane = lax.broadcasted_iota(jnp.int32, q.shape, 1)
    qf = q.astype(F32) * 0.125
    one = jnp.where(lane == 0, 1.0, 0.0)
    heads = [jnp.where(lane < 64, qf, 0.0), jnp.where(lane < 64, 0.0, qf)]
    return jnp.concatenate([jnp.concatenate([h, one], axis=1) for h in heads], axis=0).astype(BF)


def wide_grads(do, ctx):
    lane = lax.broadcasted_iota(jnp.int32, do.shape, 1)
    do = do.astype(F32)
    prod = do * ctx.astype(F32)
    out = []
    for h in range(2):
        mine = (lane < 64) if h == 0 else (lane >= 64)
        d = -jnp.sum(jnp.where(mine, prod, 0.0), axis=1, keepdims=True)
        hi = d.astype(BF).astype(F32)
        mid = (d - hi).astype(BF).astype(F32)
        low = d - hi - mid
        aug = jnp.where(lane == 0, hi, jnp.where(lane == 1, mid, jnp.where(lane == 2, low, 0.0)))
        out.append(jnp.concatenate([jnp.where(mine, do, 0.0), aug], axis=1))
    return jnp.concatenate(out, axis=0).astype(BF)


def attn_specs(rows, prompt, blocks):
    def col(n):
        return pl.BlockSpec((n, 128), lambda i, l: (0, i))

    logs = pl.BlockSpec((1, blocks, 8, CLEN), lambda i, l: (i, 0, 0, 0))
    return col(rows), col(prompt), logs


class Weight:
    def __init__(self, me, own, spots, view, sems):
        self.me, self.own, self.spots, self.view = me, own, spots, view
        self.send, self.recv = sems

    def side(self):
        return remote(self.own, self.spots(1), self.send.at[0], self.recv.at[0], self.me.core)

    def across(self):
        p = self.me.p
        return remote(self.view(None, p), self.view(2, p), self.send.at[1], self.recv.at[1], self.me.x)

    def pair(self):
        p = self.me.p
        return remote(self.view(2, p), self.view(2, p), self.send.at[2], self.recv.at[2], self.me.y)

    def over(self, which):
        h = self.me.p if which == 0 else 1 - self.me.p
        return remote(self.view(2, h), self.view(3, h), self.send.at[3 + which], self.recv.at[3 + which], self.me.core)

    def start(self):
        self.side().start()
        self.across().start()

    def relay(self):
        self.across().wait_recv()
        self.pair().start()
        self.over(0).start()

    def relay_pair(self):
        self.pair().wait_recv()
        self.over(1).start()

    def finish(self):
        self.side().wait()
        self.across().wait_send()
        self.pair().wait_send()
        self.over(0).wait()
        self.over(1).wait()


def norm_rows(x, gain, shift):
    x = x.astype(F32)
    centred = x - jnp.mean(x, axis=-1, keepdims=True)
    scale = lax.rsqrt(jnp.mean(centred * centred, axis=-1, keepdims=True) + EPS)
    return (centred * scale * gain + shift).astype(BF)


def front_kernel(lens, x_ref, gain_ref, shift_ref, wq, wp, wi, wo, ws,
                 q_ref, kp_ref, vp_ref, ko_ref, vo_ref, ctx_ref, lse_ref, an_ref, anp_ref, px_ref,
                 wq_all, wp_all, wi_all, wo_all, ws_all,
                 px, wv, wsv, kph, vpt, px_s, px_r, send, recv, loc):
    me = Peers()
    step = pl.program_id(0)
    rows = x_ref.shape[0]
    blocks = rows // CLEN
    prompt = px.shape[0]
    part = wq.shape[1]
    own_chunks = rows // CLEN
    chunks = prompt // CLEN

    def qkv_view(r, h):
        n = part // 2
        if r is None:
            return wq.at[:, pl.ds(h * n, n)]
        return wv.at[:, pl.ds(r * part + h * n, n)]

    def plain(own, everything):
        n = own.shape[0] // 2

        def view(r, h):
            return own.at[pl.ds(h * n, n)] if r is None else everything.at[r, pl.ds(h * n, n)]

        return view

    def weight(i, own, everything):
        return Weight(me, own, lambda r: everything.at[r], plain(own, everything), (send.at[i], recv.at[i]))

    w_qkv = Weight(me, wq, lambda r: wv.at[:, pl.ds(r * part, part)], qkv_view, (send.at[0], recv.at[0]))
    w_small = weight(1, ws, wsv)
    w_proj = weight(2, wp, wp_all)
    w_in = weight(3, wi, wi_all)
    w_out = weight(4, wo, wo_all)
    later = [w_proj, w_in, w_out]

    def keep(own, spot, i):
        return pltpu.make_async_copy(own, spot, loc.at[i])

    mine = [
        keep(wq, wv.at[:, pl.ds(0, part)], 0), keep(ws, wsv.at[0], 1), keep(wp, wp_all.at[0], 2),
        keep(wi, wi_all.at[0], 3), keep(wo, wo_all.at[0], 4), keep(wv, wq_all, 5), keep(wsv, ws_all, 6), keep(px, px_ref, 7),
    ]

    def chunk(k):
        return px.at[pl.ds(k * CLEN, CLEN)]

    def held(k):
        at = k if k < own_chunks else k - own_chunks
        return x_ref.at[pl.ds(at * CLEN, CLEN)]

    def hop(k, src, n, device):
        return remote(src, chunk(k), px_s.at[n, k], px_r.at[n, k], device)

    first = [k for k in range(chunks) if k < own_chunks]
    second = [k for k in range(chunks) if k >= own_chunks]
    low = [k for k in range(chunks) if k < chunks // 2]
    high = second + [k for k in range(chunks // 2, own_chunks)]

    def normed(k):
        anp_ref[k * CLEN : (k + 1) * CLEN, :] = norm_rows(px[k * CLEN : (k + 1) * CLEN, :], gain_ref[...], shift_ref[...])

    @pl.when(step == 0)
    def _():
        enter([me.core, me.x, me.y])

        @pl.when(me.t == 0)
        def _():
            for k in low:
                hop(k, held(k), 1, me.x).start()
            for k in reversed(first):
                hop(k, held(k), 0, me.core).start()

        @pl.when(me.t == 1)
        def _():
            for k in second:
                hop(k, held(k), 1, me.x).start()
                hop(k, held(k), 0, me.core).start()

        for w in (w_qkv, w_small):
            w.side().start()
        for i in range(5):
            mine[i].start()

        @pl.when(me.t == 1)
        def _():
            for k in reversed(first):
                hop(k, held(k), 0, me.core).wait_recv()
                if k in high:
                    hop(k, chunk(k), 1, me.x).start()

        for w in (w_qkv, w_small):
            w.across().start()
        for w in later:
            w.side().start()
        for b in range(blocks):
            an_ref[b * CLEN : (b + 1) * CLEN, :] = norm_rows(x_ref[b * CLEN : (b + 1) * CLEN, :], gain_ref[...], shift_ref[...])

        @pl.when(me.t == 0)
        def _():
            for k in first:
                px[k * CLEN : (k + 1) * CLEN, :] = x_ref[k * CLEN : (k + 1) * CLEN, :]
            for k in second:
                hop(k, held(k), 0, me.core).wait_recv()
            for k in first:
                hop(k, held(k), 0, me.core).wait_send()
            for k in low:
                hop(k, held(k), 1, me.x).wait_send()

        @pl.when(me.t == 1)
        def _():
            for k in second:
                px[k * CLEN : (k + 1) * CLEN, :] = held(k)[...]
                hop(k, held(k), 0, me.core).wait_send()
            for k in high:
                hop(k, chunk(k), 1, me.x).wait_send()

        @pl.when(me.t == 2)
        def _():
            for k in low:
                hop(k, chunk(k), 1, me.x).wait_recv()
                hop(k, chunk(k), 0, me.core).start()
            for k in high:
                hop(k, chunk(k), 0, me.core).wait_recv()
            for k in low:
                hop(k, chunk(k), 0, me.core).wait_send()

        @pl.when(me.t == 3)
        def _():
            for k in high:
                hop(k, chunk(k), 1, me.x).wait_recv()
                hop(k, chunk(k), 0, me.core).start()
            for k in low:
                hop(k, chunk(k), 0, me.core).wait_recv()
            for k in high:
                hop(k, chunk(k), 0, me.core).wait_send()

        for k in range(chunks):
            normed(k)
        w_small.relay()
        for w in (w_qkv, w_small):
            w.side().wait_recv()
        for i in range(2):
            mine[i].wait()

    @pl.when(step == 3)
    def _():
        for w in (w_qkv, w_small):
            w.over(0).wait_recv()
            w.over(1).wait_recv()
        mine[5].start()
        mine[6].start()
        mine[7].start()

    def moves(slot):
        def at(k, *steps):
            @pl.when(slot == k)
            def _():
                for s in steps:
                    s()

        at(2, w_qkv.relay, *[lambda w=w: w.across().start() for w in later])
        at(6, w_qkv.relay_pair, w_small.relay_pair)
        at(9, w_proj.relay)
        at(11, w_proj.relay_pair)
        at(13, w_in.relay)
        at(16, w_in.relay_pair)

    pick = pl.ds(pl.multiple_of(step * 128, 128), 128)
    w3 = jnp.concatenate([wv[0, pick], wv[1, pick], wv[2, pick]], axis=0)
    u = 2 * lax.div(step, 3)
    left = wsv[u, :16, pick].astype(F32)
    right = wsv[u + 1, :16, pick].astype(F32)
    spot = lax.broadcasted_iota(jnp.int32, left.shape, 0)

    def bias(k):
        return jnp.sum(jnp.where(spot == u + k, left, 0.0) + jnp.where(spot == u + 1 + k, right, 0.0), axis=0, keepdims=True)

    bq = bias(0)
    bv = bias(PIECES)
    for b in range(blocks):
        at = slice(b * CLEN, (b + 1) * CLEN)
        got = nt(an_ref[at, :], w3)
        q_ref[at, :] = (got[:, :128] + bq).astype(BF)
        ko_ref[at, :] = got[:, 128:256].astype(BF)
        vo_ref[at, :] = (got[:, 256:] + bv).astype(BF)
    for c in range(chunks):
        at = slice(c * CLEN, (c + 1) * CLEN)
        got = nt(anp_ref[at, :], w3[128:])
        kp_ref[at, :] = got[:, :128].astype(BF)
        vp_ref[at, :] = (got[:, 128:] + bv).astype(BF)

    kph[...] = wide_keys(kp_ref[...], lens[0], 0)
    ones = jnp.ones((16, prompt), BF)
    vpt[...] = jnp.concatenate([transposed(vp_ref[...]).astype(BF), ones], axis=0)

    def block(b, _):
        moves(step * blocks + b)
        at = pl.ds(pl.multiple_of(b * CLEN, CLEN), CLEN)
        q2 = wide_queries(q_ref[at, :])
        vot = jnp.concatenate([transposed(vo_ref[at, :]).astype(BF), ones[:, :CLEN]], axis=0)
        sp = nt(kph[...], q2)
        so = nt(wide_keys(ko_ref[at, :], lens[1 + b], 0), q2)
        top = jnp.maximum(jnp.max(sp, axis=0, keepdims=True), jnp.max(so, axis=0, keepdims=True))
        pp = jnp.exp(sp - top).astype(BF)
        po = jnp.exp(so - top).astype(BF)
        ot = nn(vpt[...], pp) + nn(vot, po)
        total = ot[128:129]
        ot = ot[:128] * (1.0 / total)
        logs = top + jnp.log(total)
        ctx_ref[at, :] = jnp.concatenate([ot[:64, :CLEN], ot[64:, CLEN:]], axis=0).T.astype(BF)
        lse_ref[0, b] = jnp.concatenate([logs[:, :CLEN], logs[:, CLEN:], jnp.zeros((6, CLEN), F32)], axis=0)
        return 0

    lax.fori_loop(0, blocks, block, 0)

    @pl.when(step == pl.num_programs(0) - 1)
    def _():
        w_out.relay()
        w_out.relay_pair()
        for w in [w_qkv, w_small]:
            w.side().wait_send()
            w.across().wait_send()
            w.pair().wait_send()
            w.over(0).wait_send()
            w.over(1).wait_send()
        for w in later:
            w.finish()
        for i in range(2, 8):
            mine[i].wait()


def front_call(lens, x, gain, shift, wq, wp, wi, wo, ws):
    rows, width = x.shape
    blocks = rows // CLEN
    pairs = width // 128
    r, p, logs = attn_specs(rows, PROMPT, blocks)
    cells = rows * (PROMPT + CLEN) * pairs * 2

    def whole(n):
        return pl.BlockSpec((n, width), lambda i, l: (0, 0))

    def shape(*s):
        return jax.ShapeDtypeStruct(s, BF)

    part = wq.shape[1]
    return pl.pallas_call(
        front_kernel,
        out_shape=(
            shape(rows, width), shape(PROMPT, width), shape(PROMPT, width), shape(rows, width), shape(rows, width),
            shape(rows, width), jax.ShapeDtypeStruct((pairs, blocks, 8, CLEN), F32),
            shape(rows, width), shape(PROMPT, width), shape(PROMPT, width),
            shape(3, PIECES * part, width), shape(PIECES, *wp.shape), shape(PIECES, *wi.shape),
            shape(PIECES, *wo.shape), shape(PIECES, *ws.shape),
        ),
        grid_spec=pltpu.PrefetchScalarGridSpec(
            num_scalar_prefetch=1,
            grid=(pairs,),
            in_specs=[whole(rows), whole(1), whole(1), ANY, ANY, ANY, ANY, ANY],
            out_specs=[r, p, p, r, r, r, logs, whole(rows), whole(PROMPT), ANY, ANY, ANY, ANY, ANY, ANY],
            scratch_shapes=[
                pltpu.VMEM((PROMPT, width), BF),
                pltpu.VMEM((3, PIECES * part, width), BF),
                pltpu.VMEM((PIECES,) + ws.shape, BF),
                pltpu.VMEM((PROMPT, 256), BF),
                pltpu.VMEM((144, PROMPT), BF),
                pltpu.SemaphoreType.DMA((2, PROMPT // CLEN)),
                pltpu.SemaphoreType.DMA((2, PROMPT // CLEN)),
                pltpu.SemaphoreType.DMA((5, 5)),
                pltpu.SemaphoreType.DMA((5, 5)),
                pltpu.SemaphoreType.DMA((8,)),
            ],
        ),
        compiler_params=pltpu.CompilerParams(collective_id=0, has_side_effects=True, vmem_limit_bytes=48 << 20),
        cost_estimate=pl.CostEstimate(flops=cells * 256 * 4, transcendentals=cells, bytes_accessed=4 << 20),
        name="front",
    )(lens, x, gain, shift, wq, wp, wi, wo, ws)


STAGES = 7


def chunk_rows(rows, dp):
    unit = 16 * (min(dp, NEAR) // 2)
    return -(-rows // unit) * unit


class Sums:
    def __init__(self, me, half, held, scratch):
        self.me, self.half, self.held = me, half, held
        (self.r1, self.r3, self.xr, self.yr, self.zr, self.own,
         self.core_s, self.core_r, self.xs, self.ys, self.zs, self.zrs, self.fs, self.frs, self.gs) = scratch
        self.chunks, self.rows, self.width = self.r1.shape
        self.wide = self.width // 2
        self.share = self.rows // half
        self.mine = pl.ds(pl.multiple_of(me.p * self.wide, 128), self.wide)
        self.other = pl.ds(pl.multiple_of((1 - me.p) * self.wide, 128), self.wide)

    @staticmethod
    def scratch(chunks, rows, width, half):
        def buf(*s, dtype=BF):
            return pltpu.VMEM((chunks,) + s, dtype)

        def dma(n):
            return pltpu.SemaphoreType.DMA((chunks, n))

        wide = width // 2
        return [
            buf(rows, width), buf(rows, width), buf(rows, width), buf(rows, wide),
            buf(half, rows // half, wide), buf(rows // half, wide, dtype=F32),
            dma(2), dma(2), dma(2), dma(2), dma(half), dma(half), dma(half), dma(half), dma(2),
        ]

    def from_core(self, c, i, src=None):
        into = (self.r1, self.r3)[i].at[c]
        return remote(into if src is None else src, into, self.core_s.at[c, i], self.core_r.at[c, i], self.me.core)

    def across(self, c):
        return remote(self.held(c, 2), self.xr.at[c], self.xs.at[c, 0], self.xs.at[c, 1], self.me.x)

    def pair(self, c):
        return remote(self.held(c, 0).at[:, self.other], self.yr.at[c], self.ys.at[c, 0], self.ys.at[c, 1], self.me.y)

    def rows_of(self, k):
        at = lax.rem(self.me.z + k, self.half) * self.share
        return pl.ds(pl.multiple_of(at, 16), self.share)

    def rest(self, c, k):
        return remote(self.held(c, 0).at[self.rows_of(k), self.mine], self.zr.at[c, k],
                      self.zs.at[c, k], self.zrs.at[c, k], self.me.along(k, self.half))

    def back(self, c, k):
        spot = self.xr.at[c, self.rows_of(0), self.mine]
        return remote(spot, spot, self.fs.at[c, k], self.frs.at[c, k], self.me.along(k, self.half))

    def back_pair(self, c):
        spot = self.xr.at[c, :, self.mine]
        return remote(spot, spot, self.gs.at[c, 0], self.gs.at[c, 1], self.me.y)

    def start(self, c, i, src):
        self.from_core(c, i, src).start()

    def blocks(self, body):
        def one(k, _):
            body(pl.ds(pl.multiple_of(k * self.share, 16), self.share))
            return 0

        lax.fori_loop(0, self.half, one, 0)

    def to_chip(self, c):
        self.from_core(c, 1).wait_recv()
        g2 = self.held(c, 2)

        def body(s):
            g2[s, :] = (g2[s, :].astype(F32) + self.r3[c, s, :].astype(F32)).astype(BF)

        self.blocks(body)
        self.across(c).start()

    def term(self, c, s, lanes):
        g0 = self.held(c, 0)
        return g0[s, lanes].astype(F32) + self.r1[c, s, lanes].astype(F32) + self.xr[c, s, lanes].astype(F32)

    def to_pair(self, c):
        self.from_core(c, 0).wait()
        self.across(c).wait()
        g0 = self.held(c, 0)

        def body(s):
            g0[s, self.other] = self.term(c, s, self.other).astype(BF)

        self.blocks(body)
        self.pair(c).start()

    def to_rest(self, c):
        self.pair(c).wait()
        g0 = self.held(c, 0)
        at = self.rows_of(0)
        self.own[c] = self.term(c, at, self.mine) + self.yr[c, at, :].astype(F32)

        def body(s):
            g0[s, self.mine] = (self.term(c, s, self.mine) + self.yr[c, s, :].astype(F32)).astype(BF)

        self.blocks(body)
        for k in range(1, self.half):
            self.rest(c, k).start()

    def to_back(self, c):
        total = self.own[c]
        for k in range(1, self.half):
            self.rest(c, k).wait()
            total = total + self.zr[c, k].astype(F32)
        self.xr[c, self.rows_of(0), self.mine] = total.astype(BF)
        for k in range(1, self.half):
            self.back(c, k).start()

    def to_back_pair(self, c):
        for k in range(1, self.half):
            self.back(c, k).wait()
        self.back_pair(c).start()

    def finish(self, c):
        self.back_pair(c).wait()

    def progress(self, plan, slot):
        steps = [None, self.to_chip, self.to_pair, self.to_rest, self.to_back, self.to_back_pair]
        for k in plan["order"]:
            since = slot - plan[k]
            c = lax.div(since, plan["gap"])
            due = since >= 0
            if plan["gap"] > 1:
                due = jnp.logical_and(due, lax.rem(since, plan["gap"]) == 0)

            @pl.when(jnp.logical_and(due, c < self.chunks))
            def _():
                steps[k](c)

    def finish_all(self):
        for c in range(self.chunks):
            self.finish(c)


class SmallSum:
    def __init__(self, me, half, sm, scratch):
        self.me, self.half, self.sm = me, half, sm
        self.got, self.z, self.s, self.r = scratch

    @staticmethod
    def scratch(rows, width, half):
        return [
            pltpu.VMEM((4, rows, width), F32),
            pltpu.VMEM((half, rows, width), F32),
            pltpu.SemaphoreType.DMA((4 + half,)),
            pltpu.SemaphoreType.DMA((4 + half,)),
        ]

    def copy(self, i):
        src, device = [(1, self.me.core), (3, self.me.core), (2, self.me.x), (0, self.me.y)][i]
        return remote(self.sm.at[src], self.got.at[i], self.s.at[i], self.r.at[i], device)

    def rest(self, k):
        return remote(self.sm.at[0], self.z.at[k], self.s.at[4 + k], self.r.at[4 + k], self.me.along(k, self.half))

    def start(self):
        self.copy(1).start()
        self.copy(0).start()

    def to_chip(self):
        self.copy(1).wait()
        self.sm[2] = self.sm[2] + self.got[1]
        self.copy(2).start()

    def to_pair(self):
        self.copy(0).wait()
        self.copy(2).wait()
        self.sm[0] = self.sm[0] + self.got[0] + self.got[2]
        self.copy(3).start()

    def to_rest(self):
        self.copy(3).wait()
        self.sm[0] = self.sm[0] + self.got[3]
        for k in range(1, self.half):
            self.rest(k).start()

    def finish(self):
        total = self.sm[0]
        for k in range(1, self.half):
            self.rest(k).wait()
            total = total + self.z[k]
        return total


SUB = 3
FFN_PLAN = {"gap": 2, "order": (5, 4, 3, 2, 1), 1: 6, 2: 12, 3: 14, 4: 16, 5: 18}
QKV_PLAN = {"gap": 2, "order": (5, 4, 3, 2, 1), 1: 24, 2: 30, 3: 32, 4: 34, 5: 36}
QKV_START = (21, 30)
SMALL_PLAN = (31, 33, 35, 37, 39)
PROMPT_PLAN = (33, 42)
LAST_SLOT = 43


def back_kernel(half, grid_pairs, lens, q_ref, kp_ref, vp_ref, ko_ref, vo_ref, lse_ref,
                w_any, an_any, anp_any, x_ref, px_any, ctx_ref, wp_any, wi_ref, wo_ref, bias_ref, vec_ref, dy_any,
                lo_any, ig_any, ffn_out, qkv_out, small_out,
                w_ref, an_ref, anp_ref, l_s, dy, hid, gs, g0, g2,
                kx, vx, kt_s, acc, dqt, dkt, dvt, prompt_acc, own_acc, share_s, gq, sm, qv, sums,
                came, over, tail, p_s, p_r, o_s, *scratch):
    me = Peers()
    step = pl.program_id(0)
    rows = x_ref.shape[0]
    width = an_ref.shape[1]
    blocks = rows // CLEN
    prompt = kp_ref.shape[0]
    chunks = prompt // CLEN
    part = width // PIECES
    feats = grid_pairs // 2 * 128
    per = width // part
    ffn_scratch, qkv_scratch, small_scratch = scratch[:15], scratch[15:30], scratch[30:]
    branch, gmi, gel, gp, mlp, mlpt = prompt_acc, own_acc, gq.at[0], gq.at[1], gq.at[2], share_s.at[pl.ds(0, width)]
    loads = [pltpu.make_async_copy(a, b, l_s.at[i]) for i, (a, b) in enumerate(((an_any, an_ref), (anp_any, anp_ref)))]

    def load_w(unit):
        return pltpu.make_async_copy(w_any.at[:, pl.ds(unit * feats, feats)], w_ref, l_s.at[2])

    px_parts = [(at, min(part, prompt - at)) for at in range(0, prompt, part)]
    load_px = [
        pltpu.make_async_copy(px_any.at[pl.ds(at, m)], gs.at[i, pl.ds(0, m)], l_s.at[3 + i]) for i, (at, m) in enumerate(px_parts)
    ]
    g1, c1, b_proj, ln2_g, ln2_b, b_out = (vec_ref[k : k + 1, :] for k in range(6))

    def piece_rows(r):
        return pl.ds(pl.multiple_of(r * part, 16), part)

    ffn = Sums(me, half, lambda c, r: (g0 if r == 0 else g2).at[c], ffn_scratch)
    qkv = Sums(me, half, lambda c, r: gq.at[c, piece_rows(r)], qkv_scratch)
    smalls = SmallSum(me, half, sm, small_scratch)
    n = prompt // 2
    spare = rows - n
    mine = pl.ds(pl.multiple_of(me.odd * n, 16), n)
    side = remote(share_s.at[pl.ds(pl.multiple_of((1 - me.odd) * n, 16), n)], came, p_s.at[0], p_r.at[0], me.core)
    across = remote(share_s.at[mine], over, p_s.at[1], p_r.at[1], me.x)
    end = remote(share_s.at[pl.ds(pl.multiple_of(me.odd * n, 16), spare)], tail, p_s.at[2], p_r.at[2], me.core)

    def block_rows(b):
        return slice(b * CLEN, (b + 1) * CLEN)

    def normal_of(x):
        x = x - jnp.mean(x, axis=-1, keepdims=True)
        scale = lax.rsqrt(jnp.mean(x * x, axis=-1, keepdims=True) + EPS)
        return x * scale, scale

    def norm_back(e, normal, scale):
        return scale * (e - jnp.mean(e, axis=-1, keepdims=True) - normal * jnp.mean(e * normal, axis=-1, keepdims=True))

    @pl.when(step == 0)
    def _():
        got = pltpu.make_async_copy(dy_any, dy, o_s.at[0])
        wp = pltpu.make_async_copy(wp_any, w_ref.at[pl.ds(0, 2)], l_s.at[2])
        wp.start()
        got.start()
        enter([me.core, me.x, me.y] + [me.along(k, half) for k in range(1, half)])
        wp.wait()
        for b in range(blocks):
            at = block_rows(b)
            h = x_ref[at, :].astype(F32) + nn(ctx_ref[at, :], w_ref[:2].reshape(width, width)) + b_proj
            hid[at, :] = h
            normal, _ = normal_of(h)
            m = (normal * ln2_g + ln2_b).astype(BF)
            mlp[at, :] = m
            mlpt[:, at] = transposed(m).astype(BF)
        got.wait()
        for c in loads:
            c.start()
        branch[...] = jnp.zeros_like(branch)
        gmi[...] = jnp.zeros_like(gmi)
        sums[...] = jnp.zeros_like(sums)

    def ffn_block(b):
        at = pl.ds(pl.multiple_of(b * CLEN, CLEN), CLEN)
        r = PIECES - 1 - step
        wi = wi_ref[0]
        wo = wo_ref[0]
        pre = nn(mlp[at, :], wi) + bias_ref[r, 16:17, :].astype(F32)
        cdf = 0.5 * (1.0 + lax.erf(pre * (0.5**0.5)))
        pdf = jnp.exp(-0.5 * pre * pre) * 0.3989422804014327
        g = (pre * cdf).astype(BF)
        d = (nt(dy[at, :], wo) * (cdf + pre * pdf)).astype(BF)
        gel[at, :] = g
        gp[at, :] = d
        branch[at, :] += nn(g, wo)
        gmi[at, :] += nt(d, wi)
        sums[pl.ds(r, 1), :] += jnp.sum(d.astype(F32), axis=0, keepdims=True)

    def weight_grads():
        @pl.when(step == 2)
        def _():
            for c in range(2 * per):
                ffn.from_core(c, 1, gs.at[c]).wait_send()

        def one(j, _):
            two = pl.ds(pl.multiple_of(j * 2 * part, 128), 2 * part)
            both = (nn(mlpt[two, :], gp[...]), tn(gel[:, two], dy[...]))
            for k, got in enumerate(both):
                got = got.astype(BF).reshape(2, part, width)
                spot = pl.ds(2 * j + k * per, 2)

                @pl.when(lax.rem(step, 2) == 0)
                def _():
                    gs[spot] = got

                @pl.when(step == 1)
                def _():
                    g2[spot] = got

                @pl.when(step == 3)
                def _():
                    g0[spot] = got

            return 0

        lax.fori_loop(0, per // 2, one, 0)
        for at, i in ((0, 1), (2, 0)):
            @pl.when(step == at)
            def _():
                for c in range(2 * per):
                    ffn.start(c, i, gs.at[c])

    def after_ffn():
        for b in range(blocks):
            at = block_rows(b)
            g = gmi[at, :]
            h = hid[at, :]
            d = dy[at, :].astype(F32)
            normal, scale = normal_of(h)
            mlp[at, :] = (h + (branch[at, :] + b_out)).astype(BF)
            gh = d + norm_back(g * ln2_g, normal, scale)
            hid[at, :] = gh
            ga = gh.astype(BF)
            gel[at, :] = ga
            for k, v in enumerate((ga.astype(F32), g * normal, g, d)):
                sums[PIECES + k : PIECES + k + 1, :] += jnp.sum(v, axis=0, keepdims=True)
            dy[at, :] = nt(ga, w_ref[:2].reshape(width, width)).astype(BF)
        load_w(1).start()
        spots = (g0.at[2 * per], gs.at[2 * per + 1], g2.at[2 * per], gs.at[2 * per])
        for r in range(0, PIECES, 2):
            got = tn(ctx_ref[:, r * part : (r + 2) * part], gel[...]).astype(BF)
            spots[r][...] = got[:part]
            spots[r + 1][...] = got[part:]
        ffn.start(2 * per, 1, gs.at[2 * per])
        ffn.start(2 * per, 0, gs.at[2 * per + 1])
        pltpu.make_async_copy(mlp, lo_any, o_s.at[1]).start()
        own_acc[...] = jnp.zeros_like(own_acc)
        prompt_acc[...] = jnp.zeros_like(prompt_acc)

    sp = step - PIECES
    spot = lax.rem(jnp.maximum(sp, 0), grid_pairs // 2)
    pair = lax.rem(jnp.maximum(sp, 0) + grid_pairs // 2, grid_pairs)
    lanes = pl.ds(pl.multiple_of(pair * 128, 128), 128)
    attending = jnp.logical_and(sp >= 0, sp < grid_pairs)

    @pl.when(attending)
    def _():
        acc[...] = jnp.zeros_like(acc)
        kx[:prompt] = wide_keys(kp_ref[...], lens[0], 0)
        vx[:prompt] = wide_values(vp_ref[...])
        vx[prompt:] = wide_values(vo_ref[...])
        kt_s[:, :prompt] = transposed(kp_ref[...]).astype(BF)
        kt_s[:, prompt:] = transposed(ko_ref[...]).astype(BF)
        for b in range(blocks):
            at = block_rows(b)
            kx[prompt + b * CLEN : prompt + (b + 1) * CLEN] = wide_keys(ko_ref[at, :], lens[1 + b], 0)

    def block(b):
        at = pl.ds(pl.multiple_of(b * CLEN, CLEN), CLEN)
        own = pl.ds(pl.multiple_of(prompt + b * CLEN, CLEN), CLEN)
        q = q_ref[at, :]
        do = dy[at, lanes]
        q2 = wide_queries(q)
        do2 = wide_grads(do, ctx_ref[at, lanes])
        qt = transposed(q).astype(BF)
        dot = transposed(do).astype(BF)
        logs = jnp.concatenate([lse_ref[0, b, 0:1, :], lse_ref[0, b, 1:2, :]], axis=1)

        def scores(keys):
            p = jnp.exp(nt(kx[keys, :], q2) - logs)
            ds = (p * nt(vx[keys, :], do2)).astype(BF)
            p = p.astype(BF)
            parts = []
            for left, m in ((qt, ds), (dot, p)):
                parts.append([nt(left[64 * h : 64 * h + 64], m[:, h * CLEN : (h + 1) * CLEN]) for h in range(2)])
            return parts, nn(kt_s[:, keys], ds)

        (dk, dv), dq = scores(pl.ds(0, prompt))
        for h in range(2):
            rows_h = slice(64 * h, 64 * h + 64)
            acc[0, rows_h, :] += dk[h]
            acc[1, rows_h, :] += dv[h]
        (dk, dv), dq_own = scores(own)
        dkt[spot, :, own] = (jnp.concatenate(dk, axis=0) * 0.125).astype(BF)
        dvt[spot, :, own] = jnp.concatenate(dv, axis=0).astype(BF)
        dq = dq + dq_own
        dqt[spot, :, at] = (jnp.concatenate([dq[:64, :CLEN], dq[64:, CLEN:]], axis=0) * 0.125).astype(BF)

        @pl.when(b == blocks - 1)
        def _():
            dkt[spot, :, :prompt] = (acc[0] * 0.125).astype(BF)
            dvt[spot, :, :prompt] = acc[1].astype(BF)

    def sub_step(sub, _):
        slot = step * SUB + sub
        ffn.progress(FFN_PLAN, slot)

        def at(k, body):
            @pl.when(slot == k)
            def _():
                body()

        def qkv_start(i):
            for c in range(3):
                qkv.start(c, i, gq.at[c, piece_rows(1 + 2 * i)])

        def prompt_chip():
            side.wait()
            share_s[mine, :] = (share_s[mine, :].astype(F32) + came[...].astype(F32)).astype(BF)

            @pl.when(me.t >= 2)
            def _():
                across.start()

        def qkv_sent():
            for c in range(3):
                qkv.from_core(c, 1, gq.at[c, piece_rows(3)]).wait_send()

        at(QKV_START[0], lambda: qkv_start(1))
        at(QKV_START[1], lambda: qkv_start(0))
        at(QKV_START[1], qkv_sent)
        qkv.progress(QKV_PLAN, slot)
        at(SMALL_PLAN[0], smalls.start)
        at(SMALL_PLAN[1], smalls.to_chip)
        at(SMALL_PLAN[2], smalls.to_pair)
        at(SMALL_PLAN[3], smalls.to_rest)
        at(PROMPT_PLAN[0], prompt_chip)

        @pl.when(step < PIECES)
        def _():
            ffn_block(sub)

        @pl.when(attending)
        def _():
            block(sub)

        return 0

    lax.fori_loop(0, SUB, sub_step, 0)

    @pl.when(step < PIECES)
    def _():
        weight_grads()

    @pl.when(step == PIECES - 1)
    def _():
        after_ffn()

    @pl.when(jnp.logical_and(attending, spot == grid_pairs // 2 - 1))
    def _():
        late = sp < grid_pairs // 2

        @pl.when(late)
        def _():
            for c in loads + [pltpu.make_async_copy(mlp, lo_any, o_s.at[1])]:
                c.wait()

        load_w(0).wait()
        dq, dk, dv = (r[...].reshape(feats, -1) for r in (dqt, dkt, dvt))
        an = an_ref[...]
        anp = anp_ref[...]
        for j, d in enumerate((dq, dk, dv)):
            g = nn(d, an) if j == 0 else nn(d[:, prompt:], an) + nn(d[:, :prompt], anp)
            gq[j, pl.ds(pl.multiple_of(jnp.where(late, feats, 0), 16), feats), :] = g.astype(BF)
        sum_q = jnp.sum(dq.astype(F32), axis=1, keepdims=True)
        sum_v = jnp.sum(dv.astype(F32), axis=1, keepdims=True)
        both = jnp.concatenate([jnp.broadcast_to(sum_q, (feats, 128)), jnp.broadcast_to(sum_v, (feats, 128))], axis=1).T
        unit_lanes = pl.ds(pl.multiple_of(jnp.where(late, feats, 0), 128), feats)
        qv[0:1, unit_lanes] = both[0:1]
        qv[1:2, unit_lanes] = both[128:129]
        def turned(ref, at, j):
            return tn(ref[:, :, at : at + CLEN].reshape(feats, CLEN), w_ref[j])

        for b in range(blocks):
            at = b * CLEN
            own_acc[at : at + CLEN, :] += (
                turned(dqt, at, 0) + turned(dkt, prompt + at, 1) + turned(dvt, prompt + at, 2)
            )
        for c in range(chunks):
            at = c * CLEN
            prompt_acc[at : at + CLEN, :] += turned(dkt, at, 1) + turned(dvt, at, 2)

        @pl.when(late)
        def _():
            load_w(0).start()

        @pl.when(jnp.logical_not(late))
        def _():
            for c in load_px:
                c.start()

    @pl.when(sp == grid_pairs - 1)
    def _():
        for c in range(chunks):
            at = block_rows(c)
            share_s[at, :] = prompt_acc[at, :].astype(BF)
        side.start()
        sum_g = jnp.zeros((1, width), F32)
        sum_c = jnp.zeros((1, width), F32)
        raws = [(own_acc, at, m, x_ref.at[pl.ds(at, m)]) for at, m in [(part * k, part) for k in range(rows // part)]]
        raws += [(prompt_acc, at, m, gs.at[i, pl.ds(0, m)]) for i, (at, m) in enumerate(px_parts)]
        for i, (grad, at, m, raw) in enumerate(raws):
            if grad is prompt_acc:
                load_px[i - rows // part].wait()
            normal, _ = normal_of(raw[...].astype(F32))
            g = grad[at : at + m, :]
            sum_g = sum_g + jnp.sum(g * normal, axis=0, keepdims=True)
            sum_c = sum_c + jnp.sum(g, axis=0, keepdims=True)
        for r in range(PIECES):
            sm[r] = jnp.zeros_like(sm[r])
            sm[r, 0:1, :] = sums[r : r + 1, :]
            sm[r, 1:5, :] = sums[PIECES : PIECES + 4, :]
            for i in range(2):
                row = qv[i : i + 1, :]
                sm[r, 8 + i : 9 + i, :] = row if r == 0 else pltpu.roll(row, width - r * part, 1)
            sm[r, 10:11, :] = sum_g
            sm[r, 11:12, :] = sum_c

    @pl.when(step == pl.num_programs(0) - 1)
    def _():
        ffn.finish_all()
        qkv.finish_all()
        outs = [(ffn.xr, ffn_out), (qkv.xr, qkv_out)]
        copies = [pltpu.make_async_copy(a, b, o_s.at[2 + i]) for i, (a, b) in enumerate(outs)]
        for c in copies:
            c.start()
        small_out[...] = smalls.finish()
        ffn.from_core(2 * per, 1, gs.at[2 * per]).wait_send()

        @pl.when(me.t >= 2)
        def _():
            across.wait_send()

        @pl.when(me.t < 2)
        def _():
            across.wait_recv()
            share_s[mine, :] = (share_s[mine, :].astype(F32) + over[...].astype(F32)).astype(BF)

        @pl.when(me.t == 1)
        def _():
            end.start()
            for at in range(0, n - spare, CLEN):
                own_acc[at : at + CLEN, :] += share_s[n + spare + at : n + spare + at + CLEN, :].astype(F32)
            end.wait_send()

        @pl.when(me.t == 0)
        def _():
            for at in range(0, n, CLEN):
                own_acc[at : at + CLEN, :] += share_s[at : at + CLEN, :].astype(F32)
            end.wait_recv()
            own_acc[n:, :] += tail[...].astype(F32)

        for b in range(blocks):
            at = block_rows(b)
            normal, scale = normal_of(x_ref[at, :].astype(F32))
            hid[at, :] += norm_back(own_acc[at, :] * g1, normal, scale)
        last = pltpu.make_async_copy(hid, ig_any, o_s.at[0])
        last.start()
        for c in copies + [last]:
            c.wait()


def back_call(lens, q, kp, vp, ko, vo, lse, wq_all, an, anp, x, px, ctx, wp, wi_all, wo_all, ws_all, vec, dy):
    rows, width = q.shape
    prompt = kp.shape[0]
    blocks = rows // CLEN
    pairs = width // 128
    part = width // PIECES
    half = min(lax.axis_size("dp"), NEAR) // 2
    cells = rows * (prompt + CLEN) * pairs * 2
    n_ffn = 2 * (width // part) + 1
    steps = -(-LAST_SLOT // SUB)
    assert blocks == SUB and wi_all.shape[1:] == (width, width) and part % (16 * half) == 0
    small_n = 16

    def pair(i):
        return lax.rem(jnp.clip(i - PIECES, 0, pairs - 1) + pairs // 2, pairs)

    def col(n):
        return pl.BlockSpec((n, 128), lambda i, l: (0, pair(i)))

    def whole(*s):
        return pl.BlockSpec(s, lambda i, l: (0,) * len(s), pipeline_mode=pl.Buffered(1))

    r, p = col(rows), col(prompt)
    logs = pl.BlockSpec((1, blocks, 8, CLEN), lambda i, l: (pair(i), 0, 0, 0))
    ff = pl.BlockSpec((1, width, width), lambda i, l: (jnp.maximum(PIECES - 1 - i, 0), 0, 0), pipeline_mode=pl.Buffered(1))
    return pl.pallas_call(
        functools.partial(back_kernel, half, pairs),
        out_shape=(
            jax.ShapeDtypeStruct((rows, width), BF),
            jax.ShapeDtypeStruct((rows, width), F32),
            jax.ShapeDtypeStruct((n_ffn, part, width), BF),
            jax.ShapeDtypeStruct((3, part, width), BF),
            jax.ShapeDtypeStruct((small_n, width), F32),
        ),
        grid_spec=pltpu.PrefetchScalarGridSpec(
            num_scalar_prefetch=1,
            grid=(steps,),
            in_specs=[r, p, p, r, r, logs, ANY, ANY, ANY, whole(rows, width),
                      ANY, whole(rows, width), ANY, ff, ff,
                      whole(*ws_all.shape), whole(*vec.shape), ANY],
            out_specs=[ANY, ANY, ANY, ANY, pl.BlockSpec((small_n, width), lambda i, l: (0, 0))],
            scratch_shapes=[
                pltpu.VMEM((3, width // 2, width), BF),
                pltpu.VMEM((rows, width), BF),
                pltpu.VMEM((prompt, width), BF),
                pltpu.SemaphoreType.DMA((3 + -(-prompt // part),)),
                pltpu.VMEM((rows, width), BF),
                pltpu.VMEM((rows, width), F32),
                pltpu.VMEM((n_ffn + 1, part, width), BF),
                pltpu.VMEM((n_ffn, part, width), BF),
                pltpu.VMEM((n_ffn, part, width), BF),
                pltpu.VMEM((prompt + rows, 256), BF),
                pltpu.VMEM((prompt + rows, 256), BF),
                pltpu.VMEM((128, prompt + rows), BF),
                pltpu.VMEM((2, 128, prompt), F32),
                pltpu.VMEM((pairs // 2, 128, rows), BF),
                pltpu.VMEM((pairs // 2, 128, prompt + rows), BF),
                pltpu.VMEM((pairs // 2, 128, prompt + rows), BF),
                pltpu.VMEM((prompt, width), F32),
                pltpu.VMEM((rows, width), F32),
                pltpu.VMEM((prompt, width), BF),
                pltpu.VMEM((3, width, width), BF),
                pltpu.VMEM((PIECES, small_n, width), F32),
                pltpu.VMEM((8, width), F32),
                pltpu.VMEM((8, width), F32),
                pltpu.VMEM((prompt // 2, width), BF),
                pltpu.VMEM((prompt // 2, width), BF),
                pltpu.VMEM((rows - prompt // 2, width), BF),
                pltpu.SemaphoreType.DMA((3,)),
                pltpu.SemaphoreType.DMA((3,)),
                pltpu.SemaphoreType.DMA((4,)),
            ]
            + Sums.scratch(n_ffn, part, width, half)
            + Sums.scratch(3, part, width, half)
            + SmallSum.scratch(small_n, width, half),
        ),
        compiler_params=pltpu.CompilerParams(collective_id=1, has_side_effects=True, vmem_limit_bytes=63 << 20),
        cost_estimate=pl.CostEstimate(flops=cells * 256 * 10, transcendentals=cells, bytes_accessed=16 << 20),
        name="back",
    )(lens, q, kp, vp, ko, vo, lse, wq_all, an, anp, x, px, ctx, wp, wi_all, wo_all, ws_all, vec, dy)


def shards(layer_in, prompt_len, cont_len, w_qkv, b_qv, w_proj, b_proj, ln1_gain, ln1_bias,
           ln2_gain, ln2_bias, w_in, b_in, w_out, b_out, out_grad):
    rows, width = layer_in.shape
    blocks = rows // CLEN
    part = w_qkv.shape[2]
    t = lax.axis_index("tensor")
    g1, c1 = (v.astype(F32)[None] for v in (ln1_gain, ln1_bias))

    group = t * blocks + jnp.arange(blocks)
    conts = group - PROMPT // CLEN
    own_len = jnp.where(conts >= 0, cont_len[0][jnp.clip(conts, 0, CONT - 1)], 0)
    lens = jnp.concatenate([prompt_len, own_len]).astype(jnp.int32)

    bias_rows = [jnp.pad(b_qv[i : i + 1], ((0, 0), (r * part, width - (r + 1) * part))) for i in range(2) for r in range(PIECES)]
    small = jnp.concatenate(bias_rows + [jnp.zeros((8, width), BF), b_in[None], jnp.zeros((15, width), BF)], axis=0)
    row = lax.broadcasted_iota(jnp.int32, (8, 1), 0)
    vec = jnp.zeros((8, width), F32)
    for k, v in enumerate((ln1_gain, ln1_bias, b_proj, ln2_gain, ln2_bias, b_out)):
        vec = jnp.where(row == k, v.astype(F32)[None], vec)
    (q, kp, vp, ko, vo, ctx, lse, attn_input, prompt_input, prompt_rows, wq_all, wp_all, wi_all, wo_all, ws_all) = front_call(
        lens, layer_in, g1, c1, w_qkv.transpose(0, 2, 1), w_proj, w_in, w_out, small
    )
    layer_out, in_grad, ffn, qkv, small = back_call(
        lens, q, kp, vp, ko, vo, lse, wq_all, attn_input, prompt_input, layer_in, prompt_rows, ctx,
        wp_all.reshape(2, width // 2, width), wi_all, wo_all, ws_all, vec, out_grad
    )
    ffn = beyond(ffn.astype(F32))
    qkv = beyond(qkv.astype(F32))
    small = beyond(small)
    per = ffn.shape[0] // 2
    grad_w_in = ffn[:per].reshape(width, -1)
    grad_w_out = ffn[per : 2 * per].reshape(-1, width)
    return (layer_out, in_grad, qkv.transpose(0, 2, 1), small[8:10, :part], ffn[2 * per], small[1], small[10], small[11],
            small[2], small[3], grad_w_in, small[0, : w_in.shape[1]], grad_w_out, small[4])


def solution(mesh):
    in_specs = (
        P(("dp", "tensor"), None),
        P("dp"),
        P("dp", None),
        P(None, None, "tensor"),
        P(None, "tensor"),
        P("tensor", None),
        P(),
        P(),
        P(),
        P(),
        P(),
        P(None, "tensor"),
        P("tensor"),
        P("tensor", None),
        P(),
        P(("dp", "tensor"), None),
    )
    out_specs = (
        P(("dp", "tensor"), None),
        P(("dp", "tensor"), None),
        P(None, None, "tensor"),
        P(None, "tensor"),
        P("tensor", None),
        P(),
        P(),
        P(),
        P(),
        P(),
        P(None, "tensor"),
        P("tensor"),
        P("tensor", None),
        P(),
    )
    return jax.shard_map(shards, mesh=mesh, in_specs=in_specs, out_specs=out_specs, check_vma=False)
```

profile of v0, /device:TPU:0, one launch (start us, length us, event | category | flops | bytes accessed | tf_op | source)
XLA Modules:
  0.0 289.9 jit_solution(16064085807514443825)
XLA Ops:
  1.4 0.8 fusion.3
  2.1 0.7 broadcast_in_dim.96
  2.8 0.7 broadcast_in_dim.93.gain_ref
  3.5 0.7 broadcast_in_dim.94.shift_ref
  4.2 0.6 gather_fusion
  4.9 0.7 convert_element_type.41
  5.6 0.7 convert_element_type.40
  6.3 0.7 convert_element_type.39
  7.0 0.7 convert_element_type.38
  7.7 0.7 convert_element_type.36
  8.4 0.7 convert_element_type.37
  9.0 0.7 select_select_fusion.vec_ref
  9.7 0.1 fusion.2
  9.8 0.2 concatenate.7.ws
  10.1 1.2 copy-done.1
  11.2 1.0 copy-done.2
  12.2 84.0 %front.1 = (bf16[768,768]{1,0:T(8,128)(2,1)S(1)}, bf16[1024,768]{1,0:T(8,128)(2,1)}, bf16[1024,768]{1,0:T(8,128)(2,1)}, bf16[768,768]{1,0:T(8,128)(2,1)S(1)}, bf...) custom-call(s32[4]{0:T(128)S(1)} %pad_add_fusion.lens, ...), custom_call_target="tpu_custom_call" | custom-call | flops 12079595520 | bytes 4194304 | tf_op jit(solution)/shard_map/front/pallas_call | solution.py:445
  96.2 1.0 copy-done.4
  97.2 1.0 copy-done.5
  98.2 1.0 copy-done.6
  99.2 0.7 copy-done.7
  99.9 0.7 copy-done.8
  100.6 177.2 %back.1 = (bf16[768,768]{1,0:T(8,128)(2,1)}, f32[768,768]{1,0:T(8,128)}, bf16[9,192,768]{2,1,0:T(8,128)(2,1)}, bf16[3,192,768]{2,1,0:T(8,128)(2,1)}, f32[16,768]{1,0:T(8,128)}) custom-call(s32[4]{0:T(128)} %copy-done.3, bf16[768,768]{1,0:T(8,128)(2,1)} %copy-done.4, bf16[1024,768]{1,0:T(8,128)(2,1)} %get-tuple-element.35.kp_ref, ...), custom_call_target="tpu_custom_call" | custom-call | flops 30198988800 | bytes 16777216 | tf_op jit(solution)/shard_map/back/pallas_call | solution.py:1081
  277.7 1.4 slice.47
  279.2 1.6 slice_reduce_fusion
  280.8 2.5 convert_bitcast_fusion
  283.3 2.6 fusion.1
  285.9 0.5 convert_element_type.42
  286.4 0.9 slice_bitcast_fusion
  287.3 1.0 copy.33
  288.3 0.2 copy-done.10
  288.4 1.4 copy.34
  (25 shorter events, 0.2 us)
Async XLA Ops:
  0.6 0.7 copy-start
  4.9 91.2 %copy-start.3 = (s32[4]{0:T(128)}, s32[4]{0:T(128)S(1)}, u32[]{:S(2)}) copy-start(s32[4]{0:T(128)S(1)} %pad_add_fusion.lens) | copy-start | bytes 52
  10.0 1.2 copy-start.1
  11.2 1.0 copy-start.2
  96.2 1.0 copy-start.4
  97.2 1.0 copy-start.5
  98.2 1.0 copy-start.6
  99.2 0.7 copy-start.7
  99.9 0.7 copy-start.8
  277.7 5.6 %copy-start.9 = (bf16[9,192,768]{2,1,0:T(8,128)(2,1)S(1)}, bf16[9,192,768]{2,1,0:T(8,128)(2,1)}, u32[]{:S(2)}) copy-start(bf16[9,192,768]{2,1,0:T(8,128)(2,1)} %get-tuple-element.53) | copy-start | bytes 7962628
  285.9 1.4 copy-start.11
  286.4 2.1 copy-start.10
where the time goes:
time: 291 us; the launch traced here: 290 us
  Pallas kernels  261 us (90%)
  local copies, waits for them, and re-layouts  19.4 us (7%)
  other arithmetic  7.91 us (3%)
    pallas_call x1, Pallas kernels, back_call(): pl.pallas_call(functools.partial(back_kernel, half, pairs), out_shape=(ja...  177 us
    pallas_call x1, Pallas kernels, front_call(): pl.pallas_call(front_kernel, out_shape=(shape(rows, width), shape(PROMPT,...  84 us
    unnamed x26, local copies, waits for them, and re-layouts  9.11 us

commit v1 on v0

--- a/solution.py
+++ b/solution.py
@@ -141,15 +141,19 @@
 
 def attn_specs(rows, prompt, blocks):
     def col(n):
-        return pl.BlockSpec((n, 128), lambda i, l: (0, i))
-
-    logs = pl.BlockSpec((1, blocks, 8, CLEN), lambda i, l: (i, 0, 0, 0))
+        return pl.BlockSpec((n, 128), lambda i, *l: (0, i))
+
+    logs = pl.BlockSpec((1, blocks, 8, CLEN), lambda i, *l: (i, 0, 0, 0))
     return col(rows), col(prompt), logs
 
+def own_length(conts, t, blocks, b):
+    c = t * blocks + b - PROMPT // CLEN
+    return jnp.where(c >= 0, conts[0, jnp.maximum(c, 0)], 0)
+
 
 class Weight:
-    def __init__(self, me, own, spots, view, sems):
-        self.me, self.own, self.spots, self.view = me, own, spots, view
+    def __init__(self, me, own, spots, view, sems, direct=False):
+        self.me, self.own, self.spots, self.view, self.direct = me, own, spots, view, direct
         self.send, self.recv = sems
 
     def side(self):
@@ -157,7 +161,8 @@
 
     def across(self):
         p = self.me.p
-        return remote(self.view(None, p), self.view(2, p), self.send.at[1], self.recv.at[1], self.me.x)
+        src, dst = (self.own, self.spots(2)) if self.direct else (self.view(None, p), self.view(2, p))
+        return remote(src, dst, self.send.at[1], self.recv.at[1], self.me.x)
 
     def pair(self):
         p = self.me.p
@@ -165,7 +170,8 @@
 
     def over(self, which):
         h = self.me.p if which == 0 else 1 - self.me.p
-        return remote(self.view(2, h), self.view(3, h), self.send.at[3 + which], self.recv.at[3 + which], self.me.core)
+        src, dst = (self.spots(2), self.spots(3)) if self.direct else (self.view(2, h), self.view(3, h))
+        return remote(src, dst, self.send.at[3 + which], self.recv.at[3 + which], self.me.core)
 
     def start(self):
         self.side().start()
@@ -173,7 +179,8 @@
 
     def relay(self):
         self.across().wait_recv()
-        self.pair().start()
+        if not self.direct:
+            self.pair().start()
         self.over(0).start()
 
     def relay_pair(self):
@@ -183,9 +190,10 @@
     def finish(self):
         self.side().wait()
         self.across().wait_send()
-        self.pair().wait_send()
         self.over(0).wait()
-        self.over(1).wait()
+        if not self.direct:
+            self.pair().wait_send()
+            self.over(1).wait()
 
 
 def norm_rows(x, gain, shift):
@@ -195,7 +203,11 @@
     return (centred * scale * gain + shift).astype(BF)
 
 
-def front_kernel(lens, x_ref, gain_ref, shift_ref, wq, wp, wi, wo, ws,
+def flat(ref):
+    return ref[...].astype(F32).reshape(1, ref.shape[0])
+
+
+def front_kernel(plen, conts, x_ref, gain_ref, shift_ref, bqv_ref, bin_ref, wq, wp, wi, wo,
                  q_ref, kp_ref, vp_ref, ko_ref, vo_ref, ctx_ref, lse_ref, an_ref, anp_ref, px_ref,
                  wq_all, wp_all, wi_all, wo_all, ws_all,
                  px, wv, wsv, kph, vpt, px_s, px_r, send, recv, loc):
@@ -226,19 +238,31 @@
         return Weight(me, own, lambda r: everything.at[r], plain(own, everything), (send.at[i], recv.at[i]))
 
     w_qkv = Weight(me, wq, lambda r: wv.at[:, pl.ds(r * part, part)], qkv_view, (send.at[0], recv.at[0]))
-    w_small = weight(1, ws, wsv)
+    w_small = weight(1, wsv.at[0], wsv)
     w_proj = weight(2, wp, wp_all)
-    w_in = weight(3, wi, wi_all)
-    w_out = weight(4, wo, wo_all)
-    later = [w_proj, w_in, w_out]
+    half_in = wi.shape[0] // 2
+    half_out = wo.shape[0] // 2
+
+    def rows_of(i, own, everything, first, n, direct=False):
+        part_rows = pl.ds(first, n)
+        sub = n // 2
+
+        def view(r, h):
+            at = pl.ds(first + h * sub, sub)
+            return own.at[at] if r is None else everything.at[r, at]
+
+        return Weight(me, own.at[part_rows], lambda r: everything.at[r, part_rows], view, (send.at[i], recv.at[i]), direct)
+
+    in_a = rows_of(3, wi, wi_all, 0, half_in)
+    in_b = rows_of(4, wi, wi_all, half_in, half_in)
+    out_a = rows_of(5, wo, wo_all, 0, half_out)
+    out_b = rows_of(6, wo, wo_all, half_out, half_out, True)
+    later = [w_proj, in_a, in_b, out_a, out_b]
 
     def keep(own, spot, i):
         return pltpu.make_async_copy(own, spot, loc.at[i])
 
-    mine = [
-        keep(wq, wv.at[:, pl.ds(0, part)], 0), keep(ws, wsv.at[0], 1), keep(wp, wp_all.at[0], 2),
-        keep(wi, wi_all.at[0], 3), keep(wo, wo_all.at[0], 4), keep(wv, wq_all, 5), keep(wsv, ws_all, 6), keep(px, px_ref, 7),
-    ]
+    mine = [keep(wq, wv.at[:, pl.ds(0, part)], 0), keep(wv, wq_all, 1), keep(wsv, ws_all, 2), keep(px, px_ref, 3)]
 
     def chunk(k):
         return px.at[pl.ds(k * CLEN, CLEN)]
@@ -256,7 +280,7 @@
     high = second + [k for k in range(chunks // 2, own_chunks)]
 
     def normed(k):
-        anp_ref[k * CLEN : (k + 1) * CLEN, :] = norm_rows(px[k * CLEN : (k + 1) * CLEN, :], gain_ref[...], shift_ref[...])
+        anp_ref[k * CLEN : (k + 1) * CLEN, :] = norm_rows(px[k * CLEN : (k + 1) * CLEN, :], flat(gain_ref), flat(shift_ref))
 
     @pl.when(step == 0)
     def _():
@@ -275,10 +299,23 @@
                 hop(k, held(k), 1, me.x).start()
                 hop(k, held(k), 0, me.core).start()
 
+        spot = lax.broadcasted_iota(jnp.int32, wsv.shape[1:], 0)
+        table = jnp.where(spot == 16, flat(bin_ref), 0.0)
+        width = wsv.shape[2]
+        for i in range(2):
+            row = jnp.concatenate([bqv_ref[i : i + 1, :].astype(F32), jnp.zeros((1, width - part), F32)], axis=1)
+            for r in range(PIECES):
+                moved = pltpu.roll(row, r * part, 1) if r else row
+                table = jnp.where(spot == i * PIECES + r, moved, table)
+        wsv[0] = table.astype(BF)
         for w in (w_qkv, w_small):
             w.side().start()
-        for i in range(5):
-            mine[i].start()
+        mine[0].start()
+
+        @pl.when(me.t >= 2)
+        def _():
+            for w in (w_qkv, w_small):
+                w.across().start()
 
         @pl.when(me.t == 1)
         def _():
@@ -287,12 +324,10 @@
                 if k in high:
                     hop(k, chunk(k), 1, me.x).start()
 
-        for w in (w_qkv, w_small):
-            w.across().start()
         for w in later:
             w.side().start()
         for b in range(blocks):
-            an_ref[b * CLEN : (b + 1) * CLEN, :] = norm_rows(x_ref[b * CLEN : (b + 1) * CLEN, :], gain_ref[...], shift_ref[...])
+            an_ref[b * CLEN : (b + 1) * CLEN, :] = norm_rows(x_ref[b * CLEN : (b + 1) * CLEN, :], flat(gain_ref), flat(shift_ref))
 
         @pl.when(me.t == 0)
         def _():
@@ -333,22 +368,24 @@
             for k in high:
                 hop(k, chunk(k), 0, me.core).wait_send()
 
+        @pl.when(me.t < 2)
+        def _():
+            for w in (w_qkv, w_small):
+                w.across().start()
+
         for k in range(chunks):
             normed(k)
-        w_small.relay()
         for w in (w_qkv, w_small):
             w.side().wait_recv()
-        for i in range(2):
-            mine[i].wait()
+        mine[0].wait()
 
     @pl.when(step == 3)
     def _():
         for w in (w_qkv, w_small):
             w.over(0).wait_recv()
             w.over(1).wait_recv()
-        mine[5].start()
-        mine[6].start()
-        mine[7].start()
+        for i in range(1, 4):
+            mine[i].start()
 
     def moves(slot):
         def at(k, *steps):
@@ -357,12 +394,18 @@
                 for s in steps:
                     s()
 
-        at(2, w_qkv.relay, *[lambda w=w: w.across().start() for w in later])
+        def go(w):
+            return lambda: w.across().start()
+
+        at(1, w_small.relay, w_qkv.relay, go(w_proj), go(in_a))
+        at(4, w_proj.relay, go(in_b))
         at(6, w_qkv.relay_pair, w_small.relay_pair)
-        at(9, w_proj.relay)
-        at(11, w_proj.relay_pair)
-        at(13, w_in.relay)
-        at(16, w_in.relay_pair)
+        at(7, in_a.relay, go(out_a))
+        at(9, w_proj.relay_pair)
+        at(11, in_b.relay, go(out_b))
+        at(13, in_a.relay_pair)
+        at(14, out_a.relay)
+        at(16, in_b.relay_pair)
 
     pick = pl.ds(pl.multiple_of(step * 128, 128), 128)
     w3 = jnp.concatenate([wv[0, pick], wv[1, pick], wv[2, pick]], axis=0)
@@ -388,7 +431,7 @@
         kp_ref[at, :] = got[:, :128].astype(BF)
         vp_ref[at, :] = (got[:, 128:] + bv).astype(BF)
 
-    kph[...] = wide_keys(kp_ref[...], lens[0], 0)
+    kph[...] = wide_keys(kp_ref[...], plen[0], 0)
     ones = jnp.ones((16, prompt), BF)
     vpt[...] = jnp.concatenate([transposed(vp_ref[...]).astype(BF), ones], axis=0)
 
@@ -398,7 +441,7 @@
         q2 = wide_queries(q_ref[at, :])
         vot = jnp.concatenate([transposed(vo_ref[at, :]).astype(BF), ones[:, :CLEN]], axis=0)
         sp = nt(kph[...], q2)
-        so = nt(wide_keys(ko_ref[at, :], lens[1 + b], 0), q2)
+        so = nt(wide_keys(ko_ref[at, :], own_length(conts, me.t, blocks, b), 0), q2)
         top = jnp.maximum(jnp.max(sp, axis=0, keepdims=True), jnp.max(so, axis=0, keepdims=True))
         pp = jnp.exp(sp - top).astype(BF)
         po = jnp.exp(so - top).astype(BF)
@@ -414,8 +457,8 @@
 
     @pl.when(step == pl.num_programs(0) - 1)
     def _():
-        w_out.relay()
-        w_out.relay_pair()
+        out_b.relay()
+        out_a.relay_pair()
         for w in [w_qkv, w_small]:
             w.side().wait_send()
             w.across().wait_send()
@@ -424,11 +467,11 @@
             w.over(1).wait_send()
         for w in later:
             w.finish()
-        for i in range(2, 8):
+        for i in range(1, 4):
             mine[i].wait()
 
 
-def front_call(lens, x, gain, shift, wq, wp, wi, wo, ws):
+def front_call(plen, conts, x, gain, shift, bqv, b_in, wq, wp, wi, wo):
     rows, width = x.shape
     blocks = rows // CLEN
     pairs = width // 128
@@ -436,12 +479,17 @@
     cells = rows * (PROMPT + CLEN) * pairs * 2
 
     def whole(n):
-        return pl.BlockSpec((n, width), lambda i, l: (0, 0))
+        return pl.BlockSpec((n, width), lambda i, *l: (0, 0))
 
     def shape(*s):
         return jax.ShapeDtypeStruct(s, BF)
 
     part = wq.shape[1]
+    small = (PIECES, 32, width)
+
+    def raw(v):
+        return pl.BlockSpec(v.shape, lambda i, *l: (0,) * v.ndim)
+
     return pl.pallas_call(
         front_kernel,
         out_shape=(
@@ -449,30 +497,30 @@
             shape(rows, width), jax.ShapeDtypeStruct((pairs, blocks, 8, CLEN), F32),
             shape(rows, width), shape(PROMPT, width), shape(PROMPT, width),
             shape(3, PIECES * part, width), shape(PIECES, *wp.shape), shape(PIECES, *wi.shape),
-            shape(PIECES, *wo.shape), shape(PIECES, *ws.shape),
+            shape(PIECES, *wo.shape), shape(*small),
         ),
         grid_spec=pltpu.PrefetchScalarGridSpec(
-            num_scalar_prefetch=1,
+            num_scalar_prefetch=2,
             grid=(pairs,),
-            in_specs=[whole(rows), whole(1), whole(1), ANY, ANY, ANY, ANY, ANY],
+            in_specs=[whole(rows), raw(gain), raw(shift), raw(bqv), raw(b_in), ANY, ANY, ANY, ANY],
             out_specs=[r, p, p, r, r, r, logs, whole(rows), whole(PROMPT), ANY, ANY, ANY, ANY, ANY, ANY],
             scratch_shapes=[
                 pltpu.VMEM((PROMPT, width), BF),
                 pltpu.VMEM((3, PIECES * part, width), BF),
-                pltpu.VMEM((PIECES,) + ws.shape, BF),
+                pltpu.VMEM(small, BF),
                 pltpu.VMEM((PROMPT, 256), BF),
                 pltpu.VMEM((144, PROMPT), BF),
                 pltpu.SemaphoreType.DMA((2, PROMPT // CLEN)),
                 pltpu.SemaphoreType.DMA((2, PROMPT // CLEN)),
-                pltpu.SemaphoreType.DMA((5, 5)),
-                pltpu.SemaphoreType.DMA((5, 5)),
-                pltpu.SemaphoreType.DMA((8,)),
+                pltpu.SemaphoreType.DMA((7, 5)),
+                pltpu.SemaphoreType.DMA((7, 5)),
+                pltpu.SemaphoreType.DMA((4,)),
             ],
         ),
-        compiler_params=pltpu.CompilerParams(collective_id=0, has_side_effects=True, vmem_limit_bytes=48 << 20),
+        compiler_params=pltpu.CompilerParams(collective_id=0, has_side_effects=True, vmem_limit_bytes=62 << 20),
         cost_estimate=pl.CostEstimate(flops=cells * 256 * 4, transcendentals=cells, bytes_accessed=4 << 20),
         name="front",
-    )(lens, x, gain, shift, wq, wp, wi, wo, ws)
+    )(plen, conts, x, gain, shift, bqv, b_in, wq, wp, wi, wo)
 
 
 STAGES = 7
@@ -677,16 +725,17 @@
 LAST_SLOT = 43
 
 
-def back_kernel(half, grid_pairs, lens, q_ref, kp_ref, vp_ref, ko_ref, vo_ref, lse_ref,
-                w_any, an_any, anp_any, x_ref, px_any, ctx_ref, wp_any, wi_ref, wo_ref, bias_ref, vec_ref, dy_any,
+def back_kernel(half, grid_pairs, plen, conts, q_ref, kp_ref, vp_ref, ko_ref, vo_ref, lse_ref,
+                w_any, an_any, anp_any, x_ref, px_any, ctx_ref, wp_any, wi_any, wo_any, wp_own, wi_own, wo_own, bias_ref,
+                g1_ref, b_proj_ref, ln2_g_ref, ln2_b_ref, b_out_ref, dy_any,
                 lo_any, ig_any, ffn_out, qkv_out, small_out,
-                w_ref, an_ref, anp_ref, l_s, dy, hid, gs, g0, g2,
+                wbuf, wp_ref, l_s, dy, hid, gs, g0, g2,
                 kx, vx, kt_s, acc, dqt, dkt, dvt, prompt_acc, own_acc, share_s, gq, sm, qv, sums,
-                came, over, tail, p_s, p_r, o_s, *scratch):
+                came, over, tail, w_s, f_s, p_s, p_r, o_s, *scratch):
     me = Peers()
     step = pl.program_id(0)
     rows = x_ref.shape[0]
-    width = an_ref.shape[1]
+    width = x_ref.shape[1]
     blocks = rows // CLEN
     prompt = kp_ref.shape[0]
     chunks = prompt // CLEN
@@ -695,16 +744,32 @@
     per = width // part
     ffn_scratch, qkv_scratch, small_scratch = scratch[:15], scratch[15:30], scratch[30:]
     branch, gmi, gel, gp, mlp, mlpt = prompt_acc, own_acc, gq.at[0], gq.at[1], gq.at[2], share_s.at[pl.ds(0, width)]
+    an_ref = wbuf.at[pl.ds(0, rows)]
+    anp_ref = wbuf.at[pl.ds(rows, prompt)]
     loads = [pltpu.make_async_copy(a, b, l_s.at[i]) for i, (a, b) in enumerate(((an_any, an_ref), (anp_any, anp_ref)))]
 
+    def w_rows(j):
+        return pl.ds(rows + prompt + j * feats, feats)
+
     def load_w(unit):
-        return pltpu.make_async_copy(w_any.at[:, pl.ds(unit * feats, feats)], w_ref, l_s.at[2])
+        return [
+            pltpu.make_async_copy(w_any.at[j, pl.ds(unit * feats, feats)], wbuf.at[w_rows(j)], w_s.at[j]) for j in range(3)
+        ]
+
+    def ffn_rows(k, j):
+        return pl.ds(pl.multiple_of((lax.rem(k, 2) * 2 + j) * width, 16), width)
+
+    def load_ffn(k, own=False):
+        srcs = (wi_own, wo_own) if own else [a.at[PIECES - 1 - k] for a in (wi_any, wo_any)]
+        return [
+            pltpu.make_async_copy(a, wbuf.at[ffn_rows(k, j)], f_s.at[lax.rem(k, 2), j]) for j, a in enumerate(srcs)
+        ]
 
     px_parts = [(at, min(part, prompt - at)) for at in range(0, prompt, part)]
     load_px = [
-        pltpu.make_async_copy(px_any.at[pl.ds(at, m)], gs.at[i, pl.ds(0, m)], l_s.at[3 + i]) for i, (at, m) in enumerate(px_parts)
+        pltpu.make_async_copy(px_any.at[pl.ds(at, m)], gs.at[i, pl.ds(0, m)], l_s.at[4 + i]) for i, (at, m) in enumerate(px_parts)
     ]
-    g1, c1, b_proj, ln2_g, ln2_b, b_out = (vec_ref[k : k + 1, :] for k in range(6))
+    g1, b_proj, ln2_g, ln2_b, b_out = (flat(v) for v in (g1_ref, b_proj_ref, ln2_g_ref, ln2_b_ref, b_out_ref))
 
     def piece_rows(r):
         return pl.ds(pl.multiple_of(r * part, 16), part)
@@ -733,22 +798,29 @@
     @pl.when(step == 0)
     def _():
         got = pltpu.make_async_copy(dy_any, dy, o_s.at[0])
-        wp = pltpu.make_async_copy(wp_any, w_ref.at[pl.ds(0, 2)], l_s.at[2])
-        wp.start()
+        first = pl.ds(0, part)
+        rest = pl.ds(part, width - part)
+        wp = [
+            pltpu.make_async_copy(wp_own, wp_ref.at[first], l_s.at[2]),
+            pltpu.make_async_copy(wp_any.at[rest], wp_ref.at[rest], l_s.at[3]),
+        ]
+        for c in wp:
+            c.start()
         got.start()
+        for c in load_ffn(0) + load_ffn(1):
+            c.start()
         enter([me.core, me.x, me.y] + [me.along(k, half) for k in range(1, half)])
-        wp.wait()
+        for c in wp:
+            c.wait()
         for b in range(blocks):
             at = block_rows(b)
-            h = x_ref[at, :].astype(F32) + nn(ctx_ref[at, :], w_ref[:2].reshape(width, width)) + b_proj
+            h = x_ref[at, :].astype(F32) + nn(ctx_ref[at, :], wp_ref[...]) + b_proj
             hid[at, :] = h
             normal, _ = normal_of(h)
             m = (normal * ln2_g + ln2_b).astype(BF)
             mlp[at, :] = m
             mlpt[:, at] = transposed(m).astype(BF)
         got.wait()
-        for c in loads:
-            c.start()
         branch[...] = jnp.zeros_like(branch)
         gmi[...] = jnp.zeros_like(gmi)
         sums[...] = jnp.zeros_like(sums)
@@ -756,8 +828,8 @@
     def ffn_block(b):
         at = pl.ds(pl.multiple_of(b * CLEN, CLEN), CLEN)
         r = PIECES - 1 - step
-        wi = wi_ref[0]
-        wo = wo_ref[0]
+        wi = wbuf[ffn_rows(step, 0), :]
+        wo = wbuf[ffn_rows(step, 1), :]
         pre = nn(mlp[at, :], wi) + bias_ref[r, 16:17, :].astype(F32)
         cdf = 0.5 * (1.0 + lax.erf(pre * (0.5**0.5)))
         pdf = jnp.exp(-0.5 * pre * pre) * 0.3989422804014327
@@ -817,8 +889,9 @@
             gel[at, :] = ga
             for k, v in enumerate((ga.astype(F32), g * normal, g, d)):
                 sums[PIECES + k : PIECES + k + 1, :] += jnp.sum(v, axis=0, keepdims=True)
-            dy[at, :] = nt(ga, w_ref[:2].reshape(width, width)).astype(BF)
-        load_w(1).start()
+            dy[at, :] = nt(ga, wp_ref[...]).astype(BF)
+        for c in loads + load_w(1):
+            c.start()
         spots = (g0.at[2 * per], gs.at[2 * per + 1], g2.at[2 * per], gs.at[2 * per])
         for r in range(0, PIECES, 2):
             got = tn(ctx_ref[:, r * part : (r + 2) * part], gel[...]).astype(BF)
@@ -839,14 +912,14 @@
     @pl.when(attending)
     def _():
         acc[...] = jnp.zeros_like(acc)
-        kx[:prompt] = wide_keys(kp_ref[...], lens[0], 0)
+        kx[:prompt] = wide_keys(kp_ref[...], plen[0], 0)
         vx[:prompt] = wide_values(vp_ref[...])
         vx[prompt:] = wide_values(vo_ref[...])
         kt_s[:, :prompt] = transposed(kp_ref[...]).astype(BF)
         kt_s[:, prompt:] = transposed(ko_ref[...]).astype(BF)
         for b in range(blocks):
             at = block_rows(b)
-            kx[prompt + b * CLEN : prompt + (b + 1) * CLEN] = wide_keys(ko_ref[at, :], lens[1 + b], 0)
+            kx[prompt + b * CLEN : prompt + (b + 1) * CLEN] = wide_keys(ko_ref[at, :], own_length(conts, me.t, blocks, b), 0)
 
     def block(b):
         at = pl.ds(pl.multiple_of(b * CLEN, CLEN), CLEN)
@@ -929,10 +1002,25 @@
 
         return 0
 
-    lax.fori_loop(0, SUB, sub_step, 0)
-
     @pl.when(step < PIECES)
     def _():
+        for c in load_ffn(step, True):
+            c.wait()
+
+    lax.fori_loop(0, SUB, sub_step, 0)
+
+    @pl.when(step < PIECES)
+    def _():
+        @pl.when(step == 0)
+        def _():
+            for c in load_ffn(2):
+                c.start()
+
+        @pl.when(step == 1)
+        def _():
+            for c in load_ffn(3, True):
+                c.start()
+
         weight_grads()
 
     @pl.when(step == PIECES - 1)
@@ -948,7 +1036,8 @@
             for c in loads + [pltpu.make_async_copy(mlp, lo_any, o_s.at[1])]:
                 c.wait()
 
-        load_w(0).wait()
+        for c in load_w(0):
+            c.wait()
         dq, dk, dv = (r[...].reshape(feats, -1) for r in (dqt, dkt, dvt))
         an = an_ref[...]
         anp = anp_ref[...]
@@ -962,7 +1051,7 @@
         qv[0:1, unit_lanes] = both[0:1]
         qv[1:2, unit_lanes] = both[128:129]
         def turned(ref, at, j):
-            return tn(ref[:, :, at : at + CLEN].reshape(feats, CLEN), w_ref[j])
+            return tn(ref[:, :, at : at + CLEN].reshape(feats, CLEN), wbuf[w_rows(j), :])
 
         for b in range(blocks):
             at = b * CLEN
@@ -975,7 +1064,8 @@
 
         @pl.when(late)
         def _():
-            load_w(0).start()
+            for c in load_w(0):
+                c.start()
 
         @pl.when(jnp.logical_not(late))
         def _():
@@ -1053,7 +1143,7 @@
             c.wait()
 
 
-def back_call(lens, q, kp, vp, ko, vo, lse, wq_all, an, anp, x, px, ctx, wp, wi_all, wo_all, ws_all, vec, dy):
+def back_call(plen, conts, q, kp, vp, ko, vo, lse, wq_all, an, anp, x, px, ctx, wp, wi_all, wo_all, wp_own, wi_own, wo_own, ws_all, vecs, dy):
     rows, width = q.shape
     prompt = kp.shape[0]
     blocks = rows // CLEN
@@ -1063,21 +1153,20 @@
     cells = rows * (prompt + CLEN) * pairs * 2
     n_ffn = 2 * (width // part) + 1
     steps = -(-LAST_SLOT // SUB)
-    assert blocks == SUB and wi_all.shape[1:] == (width, width) and part % (16 * half) == 0
+    assert blocks == SUB and wi_all.shape[1:] == (width, width) and rows == width and part % (16 * half) == 0
     small_n = 16
 
     def pair(i):
         return lax.rem(jnp.clip(i - PIECES, 0, pairs - 1) + pairs // 2, pairs)
 
     def col(n):
-        return pl.BlockSpec((n, 128), lambda i, l: (0, pair(i)))
+        return pl.BlockSpec((n, 128), lambda i, *l: (0, pair(i)))
 
     def whole(*s):
-        return pl.BlockSpec(s, lambda i, l: (0,) * len(s), pipeline_mode=pl.Buffered(1))
+        return pl.BlockSpec(s, lambda i, *l: (0,) * len(s), pipeline_mode=pl.Buffered(1))
 
     r, p = col(rows), col(prompt)
-    logs = pl.BlockSpec((1, blocks, 8, CLEN), lambda i, l: (pair(i), 0, 0, 0))
-    ff = pl.BlockSpec((1, width, width), lambda i, l: (jnp.maximum(PIECES - 1 - i, 0), 0, 0), pipeline_mode=pl.Buffered(1))
+    logs = pl.BlockSpec((1, blocks, 8, CLEN), lambda i, *l: (pair(i), 0, 0, 0))
     return pl.pallas_call(
         functools.partial(back_kernel, half, pairs),
         out_shape=(
@@ -1088,17 +1177,15 @@
             jax.ShapeDtypeStruct((small_n, width), F32),
         ),
         grid_spec=pltpu.PrefetchScalarGridSpec(
-            num_scalar_prefetch=1,
+            num_scalar_prefetch=2,
             grid=(steps,),
             in_specs=[r, p, p, r, r, logs, ANY, ANY, ANY, whole(rows, width),
-                      ANY, whole(rows, width), ANY, ff, ff,
-                      whole(*ws_all.shape), whole(*vec.shape), ANY],
-            out_specs=[ANY, ANY, ANY, ANY, pl.BlockSpec((small_n, width), lambda i, l: (0, 0))],
+                      ANY, whole(rows, width)] + [ANY] * 6 + [whole(*ws_all.shape)] + [whole(width)] * 5 + [ANY],
+            out_specs=[ANY, ANY, ANY, ANY, pl.BlockSpec((small_n, width), lambda i, *l: (0, 0))],
             scratch_shapes=[
-                pltpu.VMEM((3, width // 2, width), BF),
-                pltpu.VMEM((rows, width), BF),
-                pltpu.VMEM((prompt, width), BF),
-                pltpu.SemaphoreType.DMA((3 + -(-prompt // part),)),
+                pltpu.VMEM((max(4 * width, rows + prompt + 3 * pairs // 2 * 128), width), BF),
+                pltpu.VMEM((width, width), BF),
+                pltpu.SemaphoreType.DMA((4 + -(-prompt // part),)),
                 pltpu.VMEM((rows, width), BF),
                 pltpu.VMEM((rows, width), F32),
                 pltpu.VMEM((n_ffn + 1, part, width), BF),
@@ -1122,6 +1209,8 @@
                 pltpu.VMEM((prompt // 2, width), BF),
                 pltpu.VMEM((rows - prompt // 2, width), BF),
                 pltpu.SemaphoreType.DMA((3,)),
+                pltpu.SemaphoreType.DMA((2, 2)),
+                pltpu.SemaphoreType.DMA((3,)),
                 pltpu.SemaphoreType.DMA((3,)),
                 pltpu.SemaphoreType.DMA((4,)),
             ]
@@ -1132,34 +1221,20 @@
         compiler_params=pltpu.CompilerParams(collective_id=1, has_side_effects=True, vmem_limit_bytes=63 << 20),
         cost_estimate=pl.CostEstimate(flops=cells * 256 * 10, transcendentals=cells, bytes_accessed=16 << 20),
         name="back",
-    )(lens, q, kp, vp, ko, vo, lse, wq_all, an, anp, x, px, ctx, wp, wi_all, wo_all, ws_all, vec, dy)
+    )(plen, conts, q, kp, vp, ko, vo, lse, wq_all, an, anp, x, px, ctx, wp, wi_all, wo_all, wp_own, wi_own, wo_own, ws_all, *vecs, dy)
 
 
 def shards(layer_in, prompt_len, cont_len, w_qkv, b_qv, w_proj, b_proj, ln1_gain, ln1_bias,
            ln2_gain, ln2_bias, w_in, b_in, w_out, b_out, out_grad):
     rows, width = layer_in.shape
-    blocks = rows // CLEN
     part = w_qkv.shape[2]
-    t = lax.axis_index("tensor")
-    g1, c1 = (v.astype(F32)[None] for v in (ln1_gain, ln1_bias))
-
-    group = t * blocks + jnp.arange(blocks)
-    conts = group - PROMPT // CLEN
-    own_len = jnp.where(conts >= 0, cont_len[0][jnp.clip(conts, 0, CONT - 1)], 0)
-    lens = jnp.concatenate([prompt_len, own_len]).astype(jnp.int32)
-
-    bias_rows = [jnp.pad(b_qv[i : i + 1], ((0, 0), (r * part, width - (r + 1) * part))) for i in range(2) for r in range(PIECES)]
-    small = jnp.concatenate(bias_rows + [jnp.zeros((8, width), BF), b_in[None], jnp.zeros((15, width), BF)], axis=0)
-    row = lax.broadcasted_iota(jnp.int32, (8, 1), 0)
-    vec = jnp.zeros((8, width), F32)
-    for k, v in enumerate((ln1_gain, ln1_bias, b_proj, ln2_gain, ln2_bias, b_out)):
-        vec = jnp.where(row == k, v.astype(F32)[None], vec)
     (q, kp, vp, ko, vo, ctx, lse, attn_input, prompt_input, prompt_rows, wq_all, wp_all, wi_all, wo_all, ws_all) = front_call(
-        lens, layer_in, g1, c1, w_qkv.transpose(0, 2, 1), w_proj, w_in, w_out, small
+        prompt_len, cont_len, layer_in, ln1_gain, ln1_bias, b_qv, b_in, w_qkv.transpose(0, 2, 1), w_proj, w_in, w_out
     )
     layer_out, in_grad, ffn, qkv, small = back_call(
-        lens, q, kp, vp, ko, vo, lse, wq_all, attn_input, prompt_input, layer_in, prompt_rows, ctx,
-        wp_all.reshape(2, width // 2, width), wi_all, wo_all, ws_all, vec, out_grad
+        prompt_len, cont_len, q, kp, vp, ko, vo, lse, wq_all, attn_input, prompt_input, layer_in, prompt_rows, ctx,
+        wp_all.reshape(width, width), wi_all, wo_all, w_proj, w_in, w_out, ws_all,
+        (ln1_gain, b_proj, ln2_gain, ln2_bias, b_out), out_grad
     )
     ffn = beyond(ffn.astype(F32))
     qkv = beyond(qkv.astype(F32))

time: 291 us -> 249 us (0.86)
  Pallas kernels: 261 us -> 235 us
  local copies, waits for them, and re-layouts: 19.4 us -> 9.18 us
  other arithmetic: 7.91 us -> 3.01 us
    pallas_call x1, Pallas kernels: 177 us -> 161 us  [back_call(): pl.pallas_call(functools.partial(back_kernel, half, pairs), out_shape=(ja...]
    pallas_call x1, Pallas kernels: 84 us -> 73.9 us  [front_call(): pl.pallas_call(front_kernel, out_shape=(shape(rows, width), shape(PROMPT,...]
    unnamed x26 -> x8, local copies, waits for them, and re-layouts: 9.11 us -> 2.61 us
    convert_element_type x6 -> x0, other arithmetic: 4.1 us -> none  [the longest x4 2.74 us: shards(): vec = jnp.where(row == k, v.astype(F32)[None], vec)]
where the time goes in v1:
time: 249 us
  Pallas kernels  235 us (94%)
  local copies, waits for them, and re-layouts  9.18 us (4%)
  other arithmetic  3.01 us (1%)
    pallas_call x1, Pallas kernels, back_call(): pl.pallas_call(functools.partial(back_kernel, half, pairs), out_shape=(ja...  161 us
    pallas_call x1, Pallas kernels, front_call(): pl.pallas_call(front_kernel, out_shape=(shape(rows, width), shape(PROMPT,...  73.9 us

profile of v1, /device:TPU:0, one launch (start us, length us, event | category | flops | bytes accessed | tf_op | source)
XLA Modules:
  0.0 248.6 jit_solution(13751576220014069247)
XLA Ops:
  1.3 73.9 %front.1 = (bf16[768,768]{1,0:T(8,128)(2,1)}, bf16[1024,768]{1,0:T(8,128)(2,1)}, bf16[1024,768]{1,0:T(8,128)(2,1)}, bf16[768,768]{1,0:T(8,128)(2,1)}, bf16[768,7...) custom-call(s32[1]{0:T(128)S(6)} %copy.32.plen, ...), custom_call_target="tpu_custom_call" | custom-call | flops 12079595520 | bytes 4194304 | tf_op jit(solution)/shard_map/front/pallas_call | solution.py:493
  75.2 161.1 %back.1 = (bf16[768,768]{1,0:T(8,128)(2,1)}, f32[768,768]{1,0:T(8,128)}, bf16[9,192,768]{2,1,0:T(8,128)(2,1)}, bf16[3,192,768]{2,1,0:T(8,128)(2,1)}, f32[16,768]{1,0:T(8,128)}) custom-call(s32[1]{0:T(128)S(6)} %copy.32.plen, s32[1,8]{1,0:T(1,128)} %conts.3, bf16[768,768]{1,0:T(8,128)(2,1)} %get-tuple-element.34.q_ref, ...), custom_call_target="tpu_custom_call" | custom-call | flops 30198988800 | bytes 16777216 | tf_op jit(solution)/shard_map/back/pallas_call | solution.py:1170
  236.3 0.0 copy-start
  236.4 1.4 slice.33
  237.8 1.7 slice_reduce_fusion
  239.5 2.5 %convert_bitcast_fusion = f32[3,768,192]{1,2,0:T(8,128)} fusion(bf16[3,192,768]{2,1,0:T(8,128)(2,1)} %get-tuple-element.51), kind=kLoop, calls=%fused_computation | loop fusion | flops 442368 | bytes 2654208 | tf_op jit(solution)/shard_map/transpose | solution.py:1245
  242.0 0.0 copy-done
  242.0 2.6 %fusion = (f32[4,192,768]{2,1,0:T(8,128)}, f32[4,192,768]{2,1,0:T(8,128)}) fusion(bf16[9,192,768]{2,1,0:T(8,128)(2,1)S(1)} %copy-done), kind=kLoop, calls=%fused_computation.9 | loop fusion | bytes 9437184 | tf_op jit(solution)/shard_map/slice | solution.py:1244
  244.6 0.0 copy-start.2
  244.6 0.5 convert_element_type.4
  245.1 0.0 copy-start.1
  245.1 0.9 slice_bitcast_fusion
  246.0 0.0 copy-done.2
  246.0 1.0 copy.33
  247.0 0.2 copy-done.1
  247.2 1.4 copy.34
Async XLA Ops:
  236.3 5.6 %copy-start = (bf16[9,192,768]{2,1,0:T(8,128)(2,1)S(1)}, bf16[9,192,768]{2,1,0:T(8,128)(2,1)}, u32[]{:S(2)}) copy-start(bf16[9,192,768]{2,1,0:T(8,128)(2,1)} %get-tuple-element.53) | copy-start | bytes 7962628
  244.6 1.4 copy-start.2
  245.1 2.1 copy-start.1

commit v2 on v1

--- a/solution.py
+++ b/solution.py
@@ -717,12 +717,12 @@
 
 
 SUB = 3
-FFN_PLAN = {"gap": 2, "order": (5, 4, 3, 2, 1), 1: 6, 2: 12, 3: 14, 4: 16, 5: 18}
-QKV_PLAN = {"gap": 2, "order": (5, 4, 3, 2, 1), 1: 24, 2: 30, 3: 32, 4: 34, 5: 36}
+FFN_PLAN = {"gap": 2, "order": (5, 4, 3, 2, 1), 1: 6, 2: 12, 3: 15, 4: 18, 5: 21}
+QKV_PLAN = {"gap": 2, "order": (5, 4, 3, 2, 1), 1: 24, 2: 30, 3: 33, 4: 36, 5: 39}
 QKV_START = (21, 30)
-SMALL_PLAN = (31, 33, 35, 37, 39)
-PROMPT_PLAN = (33, 42)
-LAST_SLOT = 43
+SMALL_PLAN = (31, 34, 37, 40)
+PROMPT_PLAN = (37,)
+LAST_SLOT = 45
 
 
 def back_kernel(half, grid_pairs, plen, conts, q_ref, kp_ref, vp_ref, ko_ref, vo_ref, lse_ref,

time: 249 us -> 241 us (0.968)
  Pallas kernels: 235 us -> 227 us
    pallas_call x1, Pallas kernels: 161 us -> 154 us  [back_call(): pl.pallas_call(functools.partial(back_kernel, half, pairs), out_shape=(ja...]
where the time goes in v2:
time: 241 us
  Pallas kernels  227 us (94%)
  local copies, waits for them, and re-layouts  9.18 us (4%)
  other arithmetic  3.01 us (1%)
    pallas_call x1, Pallas kernels, back_call(): pl.pallas_call(functools.partial(back_kernel, half, pairs), out_shape=(ja...  154 us
    pallas_call x1, Pallas kernels, front_call(): pl.pallas_call(front_kernel, out_shape=(shape(rows, width), shape(PROMPT,...  73.9 us

profile of v2, /device:TPU:0, one launch (start us, length us, event | category | flops | bytes accessed | tf_op | source)
XLA Modules:
  0.0 241.0 jit_solution(7779030689018879196)
XLA Ops:
  1.3 73.9 %front.1 = (bf16[768,768]{1,0:T(8,128)(2,1)}, bf16[1024,768]{1,0:T(8,128)(2,1)}, bf16[1024,768]{1,0:T(8,128)(2,1)}, bf16[768,768]{1,0:T(8,128)(2,1)}, bf16[768,7...) custom-call(s32[1]{0:T(128)S(6)} %copy.32.plen, ...), custom_call_target="tpu_custom_call" | custom-call | flops 12079595520 | bytes 4194304 | tf_op jit(solution)/shard_map/front/pallas_call | solution.py:493
  75.2 153.5 %back.1 = (bf16[768,768]{1,0:T(8,128)(2,1)}, f32[768,768]{1,0:T(8,128)}, bf16[9,192,768]{2,1,0:T(8,128)(2,1)}, bf16[3,192,768]{2,1,0:T(8,128)(2,1)}, f32[16,768]{1,0:T(8,128)}) custom-call(s32[1]{0:T(128)S(6)} %copy.32.plen, s32[1,8]{1,0:T(1,128)} %conts.3, bf16[768,768]{1,0:T(8,128)(2,1)} %get-tuple-element.34.q_ref, ...), custom_call_target="tpu_custom_call" | custom-call | flops 30198988800 | bytes 16777216 | tf_op jit(solution)/shard_map/back/pallas_call | solution.py:1170
  228.7 0.0 copy-start
  228.8 1.4 slice.33
  230.2 1.7 slice_reduce_fusion
  231.9 2.5 %convert_bitcast_fusion = f32[3,768,192]{1,2,0:T(8,128)} fusion(bf16[3,192,768]{2,1,0:T(8,128)(2,1)} %get-tuple-element.51), kind=kLoop, calls=%fused_computation | loop fusion | flops 442368 | bytes 2654208 | tf_op jit(solution)/shard_map/transpose | solution.py:1245
  234.4 0.0 copy-done
  234.4 2.6 %fusion = (f32[4,192,768]{2,1,0:T(8,128)}, f32[4,192,768]{2,1,0:T(8,128)}) fusion(bf16[9,192,768]{2,1,0:T(8,128)(2,1)S(1)} %copy-done), kind=kLoop, calls=%fused_computation.9 | loop fusion | bytes 9437184 | tf_op jit(solution)/shard_map/slice | solution.py:1244
  237.0 0.0 copy-start.2
  237.0 0.5 convert_element_type.4
  237.5 0.0 copy-start.1
  237.5 0.9 slice_bitcast_fusion
  238.4 0.0 copy-done.2
  238.4 1.0 copy.33
  239.4 0.2 copy-done.1
  239.6 1.4 copy.34
Async XLA Ops:
  228.7 5.6 %copy-start = (bf16[9,192,768]{2,1,0:T(8,128)(2,1)S(1)}, bf16[9,192,768]{2,1,0:T(8,128)(2,1)}, u32[]{:S(2)}) copy-start(bf16[9,192,768]{2,1,0:T(8,128)(2,1)} %get-tuple-element.53) | copy-start | bytes 7962628
  237.0 1.4 copy-start.2
  237.5 2.1 copy-start.1

commit v3 on v2

--- a/solution.py
+++ b/solution.py
@@ -1102,12 +1102,8 @@
     @pl.when(step == pl.num_programs(0) - 1)
     def _():
         ffn.finish_all()
-        qkv.finish_all()
-        outs = [(ffn.xr, ffn_out), (qkv.xr, qkv_out)]
-        copies = [pltpu.make_async_copy(a, b, o_s.at[2 + i]) for i, (a, b) in enumerate(outs)]
-        for c in copies:
-            c.start()
-        small_out[...] = smalls.finish()
+        copies = [pltpu.make_async_copy(ffn.xr, ffn_out, o_s.at[2])]
+        copies[0].start()
         ffn.from_core(2 * per, 1, gs.at[2 * per]).wait_send()
 
         @pl.when(me.t >= 2)
@@ -1139,6 +1135,10 @@
             hid[at, :] += norm_back(own_acc[at, :] * g1, normal, scale)
         last = pltpu.make_async_copy(hid, ig_any, o_s.at[0])
         last.start()
+        qkv.finish_all()
+        copies.append(pltpu.make_async_copy(qkv.xr, qkv_out, o_s.at[3]))
+        copies[1].start()
+        small_out[...] = smalls.finish()
         for c in copies + [last]:
             c.wait()
 

time: 241 us -> 239 us (level)
  no operation moved by 1% of the time
where the time goes in v3:
time: 239 us
  Pallas kernels  225 us (94%)
  local copies, waits for them, and re-layouts  9.18 us (4%)
  other arithmetic  3.01 us (1%)
    pallas_call x1, Pallas kernels, back_call(): pl.pallas_call(functools.partial(back_kernel, half, pairs), out_shape=(ja...  151 us
    pallas_call x1, Pallas kernels, front_call(): pl.pallas_call(front_kernel, out_shape=(shape(rows, width), shape(PROMPT,...  73.9 us

profile of v3, /device:TPU:0, one launch (start us, length us, event | category | flops | bytes accessed | tf_op | source)
XLA Modules:
  0.0 238.9 jit_solution(7136355576356471235)
XLA Ops:
  1.3 73.9 %front.1 = (bf16[768,768]{1,0:T(8,128)(2,1)}, bf16[1024,768]{1,0:T(8,128)(2,1)}, bf16[1024,768]{1,0:T(8,128)(2,1)}, bf16[768,768]{1,0:T(8,128)(2,1)}, bf16[768,7...) custom-call(s32[1]{0:T(128)S(6)} %copy.32.plen, ...), custom_call_target="tpu_custom_call" | custom-call | flops 12079595520 | bytes 4194304 | tf_op jit(solution)/shard_map/front/pallas_call | solution.py:493
  75.2 151.4 %back.1 = (bf16[768,768]{1,0:T(8,128)(2,1)}, f32[768,768]{1,0:T(8,128)}, bf16[9,192,768]{2,1,0:T(8,128)(2,1)}, bf16[3,192,768]{2,1,0:T(8,128)(2,1)}, f32[16,768]{1,0:T(8,128)}) custom-call(s32[1]{0:T(128)S(6)} %copy.32.plen, s32[1,8]{1,0:T(1,128)} %conts.3, bf16[768,768]{1,0:T(8,128)(2,1)} %get-tuple-element.34.q_ref, ...), custom_call_target="tpu_custom_call" | custom-call | flops 30198988800 | bytes 16777216 | tf_op jit(solution)/shard_map/back/pallas_call | solution.py:1170
  226.6 0.0 copy-start
  226.7 1.4 slice.33
  228.1 1.7 slice_reduce_fusion
  229.8 2.5 %convert_bitcast_fusion = f32[3,768,192]{1,2,0:T(8,128)} fusion(bf16[3,192,768]{2,1,0:T(8,128)(2,1)} %get-tuple-element.51), kind=kLoop, calls=%fused_computation | loop fusion | flops 442368 | bytes 2654208 | tf_op jit(solution)/shard_map/transpose | solution.py:1245
  232.3 0.0 copy-done
  232.3 2.6 %fusion = (f32[4,192,768]{2,1,0:T(8,128)}, f32[4,192,768]{2,1,0:T(8,128)}) fusion(bf16[9,192,768]{2,1,0:T(8,128)(2,1)S(1)} %copy-done), kind=kLoop, calls=%fused_computation.9 | loop fusion | bytes 9437184 | tf_op jit(solution)/shard_map/slice | solution.py:1244
  234.9 0.0 copy-start.2
  234.9 0.5 convert_element_type.4
  235.4 0.0 copy-start.1
  235.4 0.9 slice_bitcast_fusion
  236.3 0.0 copy-done.2
  236.3 1.0 copy.33
  237.3 0.2 copy-done.1
  237.5 1.4 copy.34
Async XLA Ops:
  226.6 5.6 %copy-start = (bf16[9,192,768]{2,1,0:T(8,128)(2,1)S(1)}, bf16[9,192,768]{2,1,0:T(8,128)(2,1)}, u32[]{:S(2)}) copy-start(bf16[9,192,768]{2,1,0:T(8,128)(2,1)} %get-tuple-element.53) | copy-start | bytes 7962628
  234.9 1.4 copy-start.2
  235.4 2.1 copy-start.1
